TPU v7x, 128 devices: a whole 4x4x4 slice. The times are simulated.
128 devices in a mesh: pp: 2 (over core), ep: 64 (over z, y, x).
Axes of the slice: x: 4, y: 4, z: 4, core: 2. Of those that a mesh axis runs over, the one named last changes fastest.
Arguments:
- expert_out: bfloat16 [2, 64, 1536, 2048], P('pp', 'ep')
- expert_ids: int32 [2, 64, 128, 8], P('pp', 'ep')
- slot_ids: int32 [2, 64, 128, 8], P('pp', 'ep')
- gate_vals: float32 [2, 64, 128, 8], P('pp', 'ep')
- residual: bfloat16 [2, 64, 128, 2048], P('pp', 'ep')
- norm_w: float32 [2, 2048], P('pp')
- w_query: bfloat16 [2, 2048, 16, 128], P('pp')
- w_key: bfloat16 [2, 2048, 16, 128], P('pp')
- w_value: bfloat16 [2, 2048, 16, 128], P('pp')
- w_out: bfloat16 [2, 16, 128, 2048], P('pp')
Outputs:
- output: bfloat16 [2, 64, 128, 2048], P('pp', 'ep')
All inputs are finite; a program needn't handle non-finite values.
Results may differ from a plain program's by a relative error of at most 0.0133245.
Values are sent between devices in bfloat16 or wider.
A program may use at most 1 GiB of HBM per device.

v0:
```python
import jax
import jax.numpy as jnp
from jax import lax
from jax.sharding import PartitionSpec as P

NORM_EPS = 1e-6


def gated_sum(exp_table, expert_ids, slot_pos, gate_vals, residual):
    is_kept = slot_pos >= 0
    pick_rows = jax.vmap(lambda exp_rows, id_blk, pos_blk: exp_rows[id_blk, pos_blk])
    picked = pick_rows(exp_table, expert_ids, jnp.where(is_kept, slot_pos, 0))
    weight = jnp.where(is_kept, gate_vals, 0.0)
    mixed_sum = residual.astype(jnp.float32) + jnp.sum(weight[..., None] * picked.astype(jnp.float32), axis=3)
    return mixed_sum.astype(jnp.bfloat16)


def attention_block(combined, norm_w, w_query, w_key, w_value, w_out):
    y_wide = combined.astype(jnp.float32)
    inv_rms = lax.rsqrt(jnp.mean(y_wide * y_wide, axis=-1, keepdims=True) + NORM_EPS)
    x_in = (y_wide * inv_rms * norm_w).astype(jnp.bfloat16)
    q_heads = jnp.einsum('bld,dhe->blhe', x_in, w_query, preferred_element_type=jnp.float32).astype(jnp.bfloat16)
    k_heads = jnp.einsum('bld,dhe->blhe', x_in, w_key, preferred_element_type=jnp.float32).astype(jnp.bfloat16)
    v_heads = jnp.einsum('bld,dhe->blhe', x_in, w_value, preferred_element_type=jnp.float32).astype(jnp.bfloat16)
    head_dim = w_query.shape[2]
    seq_len = combined.shape[1]
    scores = jnp.einsum('bqhe,bkhe->bhqk', q_heads, k_heads, preferred_element_type=jnp.float32) * (head_dim ** -0.5)
    causal = jnp.arange(seq_len)[:, None] >= jnp.arange(seq_len)[None, :]
    attn_probs = jax.nn.softmax(jnp.where(causal, scores, -jnp.inf), axis=-1).astype(jnp.bfloat16)
    attn_out = jnp.einsum('bhqk,bkhe->bqhe', attn_probs, v_heads, preferred_element_type=jnp.float32).astype(jnp.bfloat16)
    out_proj = jnp.einsum('crif,ife->cre', attn_out, w_out, preferred_element_type=jnp.float32).astype(jnp.bfloat16)
    return (y_wide + out_proj.astype(jnp.float32)).astype(jnp.bfloat16)


def solution(mesh):
    stages = mesh.shape['pp']
    group_size = mesh.shape['ep']
    send_next = [(src_row, (src_row + 1) % stages) for src_row in range(stages)]
    tok_spec = P('pp', 'ep', None, None)
    wt_spec = P('pp', None, None, None)

    def device_step(expert_out, expert_ids, slot_ids, gate_vals, residual, norm_w, w_query, w_key, w_value, w_out):
        num_micro, seqs_dev, seq_len, d_model = residual.shape
        src_slots = expert_out.shape[2] // group_size
        returned = lax.all_to_all(expert_out, 'ep', 2, 1, tiled=True)
        block_base = lax.axis_index('ep') * src_slots
        slot_pos = jnp.where(slot_ids >= 0, slot_ids - block_base, -1)
        combined = gated_sum(returned, expert_ids, slot_pos, gate_vals, residual)
        arrived = lax.ppermute(combined, 'pp', send_next)
        flat_in = arrived.reshape(num_micro * seqs_dev, seq_len, d_model)
        result = attention_block(flat_in, norm_w[0], w_query[0], w_key[0], w_value[0], w_out[0])
        return result.reshape(num_micro, seqs_dev, seq_len, d_model)

    return jax.shard_map(device_step, mesh=mesh, in_specs=(tok_spec, tok_spec, tok_spec, tok_spec, tok_spec, P('pp', None), wt_spec, wt_spec, wt_spec, wt_spec), out_specs=tok_spec, check_vma=False)
```

profile of v0, /device:TPU:1, one launch (start us, length us, event | category | flops | bytes accessed | tf_op | source)
XLA Modules:
  0.0 277.6 jit_solution(12401802442069599530)
XLA Ops:
  0.0 12.0 %copy.55 = bf16[1,1,1536,2048]{3,1,0,2:T(2,128)(2,1)} copy(bf16[1,1,1536,2048]{3,2,1,0:T(8,128)(2,1)} %param.10) | data formatting | bytes 12582912 | tf_op args[0]
  12.0 0.5 broadcast.98
  12.6 38.9 %reduce.7 = bf16[1536,2048]{1,0:T(8,128)(2,1)} reduce(bf16[1536,1,1,2048]{3,2,1,0:T(2,128)(2,1)} %bitcast.85, bf16[]{:T(256)} %broadcast.98), dimensions={1,2}, to_apply=%bitcast.82.reduce_sub_computation | reduce | bytes 12582914
  51.4 15.3 %reshape.196 = bf16[64,2,24576]{2,1,0:T(2,128)(2,1)} reshape(bf16[1536,2048]{1,0:T(8,128)(2,1)} %reduce.7) | data formatting | bytes 12582912
  66.7 0.0 copy-start.1
  66.7 0.0 copy-start.3
  66.7 0.0 copy-start.2
  66.8 12.5 %all-to-all-start = ((bf16[64,2,24576]{2,1,0:T(2,128)(2,1)}), bf16[64,2,24576]{2,1,0:T(2,128)(2,1)}, u32[]{:S(2)}, u32[]{:S(2)}) async-start(bf16[64,2,24576]{2,1,0:T(2,128)(2,1)} %reshape.196), calls=%async_computation | async-start | bytes 12582912 | tf_op jit(solution)/shard_map/all_to_all | solution.py:45
  79.3 0.0 copy-done.1
  79.3 0.0 copy-done.3
  79.3 0.1 copy.29
  79.4 0.1 reshape.185
  79.5 0.0 copy-done.2
  79.6 0.1 copy.27
  79.7 88.5 %all-to-all-done = bf16[64,2,24576]{2,1,0:T(2,128)(2,1)} async-done(((bf16[64,2,24576]{2,1,0:T(2,128)(2,1)}), bf16[64,2,24576]{2,1,0:T(2,128)(2,1)}, u32[]{:S(2)}, u32[]{:S(2)}) %all-to-all-start) | async-done | bytes 6291488 | tf_op jit(solution)/shard_map/all_to_all | solution.py:45
  168.2 36.8 %reshape.197 = bf16[1536,1,1,2048]{3,2,1,0:T(2,128)(2,1)} reshape(bf16[64,2,24576]{2,1,0:T(2,128)(2,1)} %all-to-all-done) | data formatting | bytes 12582912
  204.9 11.2 %copy.39 = bf16[1,1,1536,2048]{3,2,0,1:T(8,128)(2,1)} copy(bf16[1,1,1536,2048]{3,1,0,2:T(2,128)(2,1)} %bitcast.84) | data formatting | bytes 12582912
  216.1 0.0 copy-start
  216.1 0.0 copy-start.4
  216.2 26.7 %gather_fusion = bf16[1024,2048]{1,0:T(8,128)(2,1)} fusion(bf16[1,64,24,2048]{3,2,1,0:T(8,128)(2,1)} %bitcast.83, s32[1024]{0:T(1024)S(1)} %reshape.185), kind=kCustom, calls=%fused_computation | custom fusion | bytes 8400896 | tf_op jit(solution)/shard_map/vmap()/gather | solution.py:11
  242.8 6.5 %fusion.1 = f32[128,2048]{1,0:T(8,128)S(1)} fusion(bf16[1024,2048]{1,0:T(8,128)(2,1)} %gather_fusion, f32[128,8]{1,0:T(8,128)S(1)} %copy.27), kind=kLoop, calls=%fused_computation.3 | loop fusion | flops 6029312 | bytes 5246976 | tf_op jit(solution)/shard_map/reduce_sum | solution.py:14
  249.4 0.0 copy-done
  249.4 0.1 fusion.39
  249.5 5.3 %collective-permute-start = (bf16[1,1,128,2048]{3,2,1,0:T(8,128)(2,1)S(1)}, bf16[1,1,128,2048]{3,2,1,0:T(8,128)(2,1)S(1)}, u32[]{:S(2)}, u32[]{:S(2)}) collective-permute-start(bf16[1,1,128,2048]{3,2,1,0:T(8,128)(2,1)S(1)} %fusion.39), channel_id=1, source_target_pairs={{0,64},{64,0},{1,65},{65,1},{2,66},{66,2},{3,67},{67,3},{4,68},{68... | collective-permute-start | bytes 1572872 | tf_op jit(solution)/shard_map/ppermute | solution.py:49
  254.8 1.5 collective-permute-done
  256.3 0.2 fusion.36
  256.5 0.0 copy-done.4
  256.5 4.9 %fusion.25 = bf16[128,16,128]{2,0,1:T(8,128)(2,1)S(1)} fusion(bf16[2048,16,128]{2,1,0:T(8,128)(2,1)} %bitcast.86, bf16[1,1,128,2048]{3,2,1,0:T(8,128)(2,1)S(1)} %collective-permute-done, f32[2048]{0:T(1024)S(1)} %bitcast.89, f32[128]{0:T(128)S(1)} %add_rsqrt_fusion), kind=kOutput, calls=%fused_computation.24 | convolution fusion | flops 1075052544 | bytes 9445888 | tf_op jit(solution)/shard_map/bld,dhe->blhe/dot_general | solution.py:22
  261.4 5.2 %fusion.21 = f32[16,128,128]{1,2,0:T(8,128)S(1)} fusion(bf16[128,16,128]{2,0,1:T(8,128)(2,1)S(1)} %fusion.25, bf16[2048,16,128]{2,1,0:T(8,128)(2,1)} %bitcast.87, pred[128,128]{0,1:T(8,128)(4,1)S(1)} %iota_compare_fusion, bf16[1,1,128,2048]{3,2,1,0:T(8,128)(2,1)S(1)} %collective-permute-done, f32[2048]{0:T(1024)S(1)} %bitcast.90, f32[128]{0:T(128)S(1)} %add_rsqrt_fusion), kind=kOutput, calls=%fused_computation.21 | convolution fusion | flops 1142685696 | bytes 10510848 | tf_op jit(solution)/shard_map/bqhe,bkhe->bhqk/dot_general | solution.py:27
  266.6 0.2 fusion.62
  266.9 4.9 %fusion.22 = bf16[128,16,128]{2,0,1:T(8,128)(2,1)S(1)} fusion(bf16[2048,16,128]{2,1,0:T(8,128)(2,1)} %bitcast.88, bf16[1,1,128,2048]{3,2,1,0:T(8,128)(2,1)S(1)} %collective-permute-done, f32[2048]{0:T(1024)S(1)} %bitcast.91, f32[128]{0:T(128)S(1)} %add_rsqrt_fusion), kind=kOutput, calls=%fused_computation.23 | convolution fusion | flops 1075052544 | bytes 9445888 | tf_op jit(solution)/shard_map/bld,dhe->blhe/dot_general | solution.py:24
  271.8 5.8 %fusion.42 = bf16[1,1,128,2048]{3,2,1,0:T(8,128)(2,1)} fusion(bf16[1,16,128,2048]{3,2,1,0:T(8,128)(2,1)} %param.19, bf16[128,16,128]{2,0,1:T(8,128)(2,1)S(1)} %fusion.22, bf16[1,1,128,2048]{3,2,1,0:T(8,128)(2,1)S(1)} %collective-permute-done, f32[16,128]{1,0:T(8,128)S(1)} %fusion.62, f32[16,128,128]{1,2,0:T(8,128)S(1)} %fusion.21), kind=kOutput, calls=%fused_computation.35 | convolution fusion | flops 1143212160 | bytes 11018240 | tf_op jit(solution)/shard_map/crif,ife->cre/dot_general | solution.py:31
  (7 shorter events, 0.1 us)
Async XLA Ops:
  66.7 12.5 %copy-start.1 = (s32[1,1,128,8]{2,3,1,0:T(8,128)S(1)}, s32[1,1,128,8]{2,3,1,0:T(8,128)}, u32[]{:S(2)}) copy-start(s32[1,1,128,8]{2,3,1,0:T(8,128)} %param.12) | copy-start | bytes 12292
  66.7 12.5 %copy-start.3 = (s32[1,1,128,8]{2,3,1,0:T(8,128)S(1)}, s32[1,1,128,8]{2,3,1,0:T(8,128)}, u32[]{:S(2)}) copy-start(s32[1,1,128,8]{2,3,1,0:T(8,128)} %param.11) | copy-start | bytes 12292
  66.7 12.8 %copy-start.2 = (f32[1,1,128,8]{2,3,1,0:T(8,128)S(1)}, f32[1,1,128,8]{2,3,1,0:T(8,128)}, u32[]{:S(2)}) copy-start(f32[1,1,128,8]{2,3,1,0:T(8,128)} %param.13) | copy-start | bytes 12292
  66.8 101.4 %all-to-all-start = ((bf16[64,2,24576]{2,1,0:T(2,128)(2,1)}), bf16[64,2,24576]{2,1,0:T(2,128)(2,1)}, u32[]{:S(2)}, u32[]{:S(2)}) async-start(bf16[64,2,24576]{2,1,0:T(2,128)(2,1)} %reshape.196), calls=%async_computation | async-start | bytes 12582912 | tf_op jit(solution)/shard_map/all_to_all | solution.py:45
  216.1 33.2 %copy-start = (bf16[1,1,128,2048]{3,2,1,0:T(8,128)(2,1)S(1)}, bf16[1,1,128,2048]{3,2,1,0:T(8,128)(2,1)}, u32[]{:S(2)}) copy-start(bf16[1,1,128,2048]{3,2,1,0:T(8,128)(2,1)} %param.14) | copy-start | bytes 1572868
  216.1 40.3 %copy-start.4 = (f32[1,2048]{1,0:T(1,128)S(1)}, f32[1,2048]{1,0:T(1,128)}, u32[]{:S(2)}) copy-start(f32[1,2048]{1,0:T(1,128)} %param.15) | copy-start | bytes 24580
  249.5 6.8 %collective-permute-start = (bf16[1,1,128,2048]{3,2,1,0:T(8,128)(2,1)S(1)}, bf16[1,1,128,2048]{3,2,1,0:T(8,128)(2,1)S(1)}, u32[]{:S(2)}, u32[]{:S(2)}) collective-permute-start(bf16[1,1,128,2048]{3,2,1,0:T(8,128)(2,1)S(1)} %fusion.39), channel_id=1, source_target_pairs={{0,64},{64,0},{1,65},{65,1},{2,66},{66,2},{3,67},{67,3},{4,68},{68... | collective-permute-start | bytes 1572872 | tf_op jit(solution)/shard_map/ppermute | solution.py:49
where the time goes:
time: 281 us; the launch traced here: 278 us
  local copies, waits for them, and re-layouts  103 us (37%)
  waiting for transfers between devices  90 us (32%)
  other arithmetic  46 us (16%)
  matrix products  20.9 us (7%)
  starting transfers between devices  17.8 us (6%)
    all_to_all x1, waiting for transfers between devices, device_step(): returned = lax.all_to_all(expert_out, 'ep', 2, 1, tiled=True)  88.5 us
    unnamed x15, local copies, waits for them, and re-layouts  75.9 us
    unnamed x1, other arithmetic  38.9 us
    gather x4, local copies, waits for them, and re-layouts, gated_sum(): exp_rows[id_blk, pos_blk]  26.9 us
    all_to_all x1, starting transfers between devices, device_step(): returned = lax.all_to_all(expert_out, 'ep', 2, 1, tiled=True)  12.5 us
    reduce_sum x1, other arithmetic, gated_sum(): jnp.sum(weight[..., None] * picked.astype(jnp.float32), axis=3)  6.53 us
    dot_general x1, matrix products, attention_block(): jnp.einsum('crif,ife->cre', attn_out, w_out, preferred_element_type=jnp.f...  5.84 us
  transfers between devices with their start and end apart: 2, of which 2 were waited for; matrix products, arithmetic and copies ran while one was open for 0% of the time, Pallas kernels for 0%

commit v1 on v0

v1 whole, which is shorter than its diff:
```python
import functools
import itertools

import jax
import jax.numpy as jnp
from jax import lax
from jax.experimental import pallas as pl
from jax.experimental.pallas import tpu as pltpu
from jax.sharding import PartitionSpec as P

NORM_EPS = 1e-6
MESH = pl.DeviceIdType.MESH
SIDE = 4
CHUNKS = 4
CLASSES = [c for c in itertools.product((0, 1), repeat=3) if any(c)]
CLASS_SIZE = [3 ** (3 - sum(c)) for c in CLASSES]
CLASS_BASE = [sum(CLASS_SIZE[:k]) for k in range(len(CLASSES))]
RELAYED = sum(CLASS_SIZE)
DIRECT = 27


def exchange_kernel(o_ref, kg_ref, h_ref, y_ref, rows, relay, kg_in, h_in, g_mat, side_sem, dir_send, dir_recv, leg1_send, leg1_recv, leg2_send):
    stage = lax.axis_index('pp')
    me = lax.axis_index('ep')
    other = 1 - stage
    pos = (me // 16, (me // 4) % 4, me % 4)
    sign = [1 - 2 * (p % 2) for p in pos]
    slots = rows.shape[2]
    width = rows.shape[3]
    seq, k_rows = g_mat.shape[0] // 3, g_mat.shape[1]

    def at(offset):
        z, y, x = [lax.rem(p + d + SIDE, SIDE) for p, d in zip(pos, offset)]
        return z * 16 + y * 4 + x

    def cube(i):
        return (i // 9 - 1, (i // 3) % 3 - 1, i % 3 - 1)

    def free_offset(cls, i):
        out = []
        for c in cls:
            if c:
                out.append(0)
            else:
                out.append(i % 3 - 1)
                i = i // 3
        return out

    barrier = pltpu.get_barrier_semaphore()

    def hello(i, carry):
        pl.semaphore_signal(barrier, inc=1, device_id=(other, at(cube(i))), device_id_type=MESH)
        return carry

    lax.fori_loop(0, DIRECT, hello, 0)
    for cls in CLASSES:
        peer = at([s * c for s, c in zip(sign, cls)])
        pl.semaphore_signal(barrier, inc=1, device_id=(stage, peer), device_id_type=MESH)
    pl.semaphore_wait(barrier, DIRECT + len(CLASSES))

    side = [
        pltpu.make_async_remote_copy(src_ref=src, dst_ref=dst, send_sem=side_sem.at[0, k], recv_sem=side_sem.at[1, k], device_id=(other, me), device_id_type=MESH)
        for k, (src, dst) in enumerate(((kg_ref, kg_in), (h_ref, h_in)))
    ]
    for copy in side:
        copy.start()

    def block(dest, f):
        return o_ref.at[dest, :, pl.ds(f * width, width)]

    def start_direct(f):
        def body(i, carry):
            dest = at(cube(i))
            pltpu.make_async_remote_copy(src_ref=block(dest, f), dst_ref=rows.at[f, me], send_sem=dir_send.at[f], recv_sem=dir_recv.at[f], device_id=(other, dest), device_id_type=MESH).start()
            return carry
        lax.fori_loop(0, DIRECT, body, 0)

    def start_leg1(f):
        for k, cls in enumerate(CLASSES):
            peer = at([s * c for s, c in zip(sign, cls)])

            def body(i, carry):
                dest = at([2 * c + o for c, o in zip(cls, free_offset(cls, i))])
                pltpu.make_async_remote_copy(src_ref=block(dest, f), dst_ref=relay.at[f, CLASS_BASE[k] + i], send_sem=leg1_send.at[f], recv_sem=leg1_recv.at[f, k], device_id=(stage, peer), device_id_type=MESH).start()
                return carry
            lax.fori_loop(0, CLASS_SIZE[k], body, 0)

    def forward(f):
        for k, cls in enumerate(CLASSES):
            source = at([s * c for s, c in zip(sign, cls)])
            held = relay.at[f, pl.ds(CLASS_BASE[k], CLASS_SIZE[k])]
            pltpu.make_async_copy(held, held, leg1_recv.at[f, k]).wait()

            def body(i, carry):
                dest = at([o - s * c for s, c, o in zip(sign, cls, free_offset(cls, i))])
                pltpu.make_async_remote_copy(src_ref=relay.at[f, CLASS_BASE[k] + i], dst_ref=rows.at[f, source], send_sem=leg2_send.at[f], recv_sem=dir_recv.at[f], device_id=(other, dest), device_id_type=MESH).start()
                return carry
            lax.fori_loop(0, CLASS_SIZE[k], body, 0)

    def build_gates():
        for copy in side:
            copy.wait_recv()
        kg = kg_in[...]
        step = 256
        for b in range(k_rows // step):
            col = (lax.broadcasted_iota(jnp.int32, (seq, step), 1) + b * step).astype(jnp.float32)
            val = jnp.zeros((seq, step), jnp.float32)
            for i in range(8):
                val = jnp.where(kg[:, i:i + 1] == col, kg[:, 8 + i:9 + i], val)
            high = val.astype(jnp.bfloat16)
            rest = val - high.astype(jnp.float32)
            mid = rest.astype(jnp.bfloat16)
            low = (rest - mid.astype(jnp.float32)).astype(jnp.bfloat16)
            for part, piece in enumerate((high, mid, low)):
                g_mat[part * seq:(part + 1) * seq, b * step:(b + 1) * step] = piece

    def combine(f):
        pltpu.make_async_copy(rows.at[f], rows.at[f], dir_recv.at[f]).wait()
        table = rows[f].reshape(k_rows, width)
        sums = jnp.dot(g_mat[...], table, preferred_element_type=jnp.float32)
        mixed = sums[:seq] + (sums[seq:2 * seq] + sums[2 * seq:])
        cols = slice(f * width, (f + 1) * width)
        y_ref[:, cols] = (h_in[:, cols].astype(jnp.float32) + mixed).astype(jnp.bfloat16)

    start_leg1(0)
    start_direct(0)
    start_leg1(1)
    start_direct(1)
    build_gates()
    forward(0)
    for f in range(2, CHUNKS):
        start_leg1(f)
        start_direct(f)
        forward(f - 1)
        combine(f - 2)
    forward(CHUNKS - 1)
    combine(CHUNKS - 2)
    combine(CHUNKS - 1)

    for copy in side:
        copy.wait_send()
    for f in range(CHUNKS):
        pltpu.make_async_copy(rows.at[f, pl.ds(0, DIRECT)], rows.at[f, pl.ds(0, DIRECT)], dir_send.at[f]).wait()
        pltpu.make_async_copy(relay.at[f], relay.at[f], leg1_send.at[f]).wait()
        pltpu.make_async_copy(relay.at[f], relay.at[f], leg2_send.at[f]).wait()


def exchange(o_tab, kg, h):
    n, slots, d = o_tab.shape
    seq = h.shape[0]
    width = d // CHUNKS
    dma = pltpu.SemaphoreType.DMA
    return pl.pallas_call(
        exchange_kernel,
        out_shape=jax.ShapeDtypeStruct((seq, d), jnp.bfloat16),
        in_specs=[pl.BlockSpec(memory_space=pl.ANY), pl.BlockSpec(memory_space=pltpu.VMEM), pl.BlockSpec(memory_space=pltpu.VMEM)],
        out_specs=pl.BlockSpec(memory_space=pltpu.VMEM),
        scratch_shapes=[
            pltpu.VMEM((CHUNKS, n, slots, width), jnp.bfloat16),
            pltpu.VMEM((CHUNKS, RELAYED, slots, width), jnp.bfloat16),
            pltpu.VMEM(kg.shape, jnp.float32),
            pltpu.VMEM((seq, d), jnp.bfloat16),
            pltpu.VMEM((3 * seq, n * slots), jnp.bfloat16),
            dma((2, 2)),
            dma((CHUNKS,)),
            dma((CHUNKS,)),
            dma((CHUNKS,)),
            dma((CHUNKS, len(CLASSES))),
            dma((CHUNKS,)),
        ],
        compiler_params=pltpu.CompilerParams(collective_id=0, has_side_effects=True, vmem_limit_bytes=60 * 1024 * 1024),
        name='exchange',
    )(o_tab, kg, h)


def attention_block(combined, norm_w, w_query, w_key, w_value, w_out):
    y_wide = combined.astype(jnp.float32)
    inv_rms = lax.rsqrt(jnp.mean(y_wide * y_wide, axis=-1, keepdims=True) + NORM_EPS)
    x_in = (y_wide * inv_rms * norm_w).astype(jnp.bfloat16)
    q_heads = jnp.einsum('bld,dhe->blhe', x_in, w_query, preferred_element_type=jnp.float32).astype(jnp.bfloat16)
    k_heads = jnp.einsum('bld,dhe->blhe', x_in, w_key, preferred_element_type=jnp.float32).astype(jnp.bfloat16)
    v_heads = jnp.einsum('bld,dhe->blhe', x_in, w_value, preferred_element_type=jnp.float32).astype(jnp.bfloat16)
    head_dim = w_query.shape[2]
    seq_len = combined.shape[1]
    scores = jnp.einsum('bqhe,bkhe->bhqk', q_heads, k_heads, preferred_element_type=jnp.float32) * (head_dim ** -0.5)
    causal = jnp.arange(seq_len)[:, None] >= jnp.arange(seq_len)[None, :]
    attn_probs = jax.nn.softmax(jnp.where(causal, scores, -jnp.inf), axis=-1).astype(jnp.bfloat16)
    attn_out = jnp.einsum('bhqk,bkhe->bqhe', attn_probs, v_heads, preferred_element_type=jnp.float32).astype(jnp.bfloat16)
    out_proj = jnp.einsum('crif,ife->cre', attn_out, w_out, preferred_element_type=jnp.float32).astype(jnp.bfloat16)
    return (y_wide + out_proj.astype(jnp.float32)).astype(jnp.bfloat16)


def solution(mesh):
    n = mesh.shape['ep']
    tok_spec = P('pp', 'ep', None, None)
    wt_spec = P('pp', None, None, None)

    def device_step(expert_out, expert_ids, slot_ids, gate_vals, residual, norm_w, w_query, w_key, w_value, w_out):
        num_micro, seqs_dev, seq_len, d_model = residual.shape
        slots = expert_out.shape[2] // n
        me = lax.axis_index('ep')
        key = jnp.where(slot_ids >= 0, expert_ids * slots + slot_ids - me * slots, -1)
        kg = jnp.concatenate([key.astype(jnp.float32), gate_vals], axis=-1).reshape(seq_len, -1)
        arrived = exchange(expert_out.reshape(n, slots, d_model), kg, residual.reshape(seq_len, d_model))
        result = attention_block(arrived.reshape(1, seq_len, d_model), norm_w[0], w_query[0], w_key[0], w_value[0], w_out[0])
        return result.reshape(num_micro, seqs_dev, seq_len, d_model)

    return jax.shard_map(device_step, mesh=mesh, in_specs=(tok_spec, tok_spec, tok_spec, tok_spec, tok_spec, P('pp', None), wt_spec, wt_spec, wt_spec, wt_spec), out_specs=tok_spec, check_vma=False)
```

time: 281 us -> 122 us (0.43)
  local copies, waits for them, and re-layouts: 103 us -> 0.74 us
  Pallas kernels: 0 us -> 94.2 us
  waiting for transfers between devices: 90 us -> 0 us
  other arithmetic: 46 us -> 2.87 us
  starting transfers between devices: 17.8 us -> 0 us
    pallas_call x0 -> x1, Pallas kernels: none -> 94.2 us  [exchange(): pl.pallas_call(exchange_kernel, out_shape=jax.ShapeDtypeStruct((seq, d),...]
    all_to_all x1 -> x0, waiting for transfers between devices: 88.5 us -> none  [device_step(): returned = lax.all_to_all(expert_out, 'ep', 2, 1, tiled=True)]
    unnamed x15 -> x4, local copies, waits for them, and re-layouts: 75.9 us -> 0.01 us
    unnamed x1 -> x0, other arithmetic: 38.9 us -> none
    gather x4 -> x0, local copies, waits for them, and re-layouts: 26.9 us -> none  [gated_sum(): exp_rows[id_blk, pos_blk]]
    all_to_all x1 -> x0, starting transfers between devices: 12.5 us -> none  [device_step(): returned = lax.all_to_all(expert_out, 'ep', 2, 1, tiled=True)]
    reduce_sum x1 -> x0, other arithmetic: 6.53 us -> none  [gated_sum(): jnp.sum(weight[..., None] * picked.astype(jnp.float32), axis=3)]
    ppermute x1 -> x0, starting transfers between devices: 5.26 us -> none  [device_step(): arrived = lax.ppermute(combined, 'pp', send_next)]
  transfers between devices with their start and end apart: 2 -> 0, of which waited for: 2 -> 0; matrix products, arithmetic and copies ran while one was open for 0% -> 0% of each run, Pallas kernels for 0% -> 0%
where the time goes in v1:
time: 122 us; the launch traced here: 121 us
  Pallas kernels  94.2 us (77%)
  matrix products  23.3 us (19%)
  other arithmetic  2.87 us (2%)
    pallas_call x1, Pallas kernels, exchange(): pl.pallas_call(exchange_kernel, out_shape=jax.ShapeDtypeStruct((seq, d),...  94.2 us
    dot_general x1, matrix products, attention_block(): jnp.einsum('bld,dhe->blhe', x_in, w_value, preferred_element_type=jnp.flo...  7.2 us
    dot_general x1, matrix products, attention_block(): jnp.einsum('crif,ife->cre', attn_out, w_out, preferred_element_type=jnp.f...  5.74 us
    dot_general x1, matrix products, attention_block(): jnp.einsum('bqhe,bkhe->bhqk', q_heads, k_heads, preferred_element_type=jn...  5.23 us
    dot_general x1, matrix products, attention_block(): jnp.einsum('bld,dhe->blhe', x_in, w_query, preferred_element_type=jnp.flo...  5.15 us

profile of v1, /device:TPU:1, one launch (start us, length us, event | category | flops | bytes accessed | tf_op | source)
XLA Modules:
  0.0 121.2 jit_solution(11351559485095694505)
XLA Ops:
  0.0 0.7 select_convert_fusion
  0.7 0.7 pad_maximum_fusion
  1.4 0.7 copy.21
  2.1 94.2 %exchange.1 = bf16[128,2048]{1,0:T(8,128)(2,1)} custom-call(bf16[64,24,2048]{2,1,0:T(8,128)(2,1)} %bitcast.54, f32[128,16]{1,0:T(8,128)} %bitcast.56, bf16[128,2048]{1,0:T(8,128)(2,1)} %bitcast.55), custom_call_target="tpu_custom_call" | custom-call | tf_op jit(solution)/shard_map/exchange/pallas_call | solution.py:153
  96.4 1.2 %fusion.42 = f32[128]{0:T(128)S(1)} fusion(bf16[128,2048]{1,0:T(8,128)(2,1)} %exchange.1), kind=kLoop, calls=%fused_computation.26 | loop fusion | flops 786304 | bytes 524800 | tf_op jit(solution)/shard_map/reduce_sum | solution.py:178
  97.6 0.0 copy-start
  97.6 0.0 copy-start.1
  97.7 5.2 %fusion.33 = bf16[128,16,128]{2,0,1:T(8,128)(2,1)S(1)} fusion(bf16[2048,16,128]{2,1,0:T(8,128)(2,1)} %bitcast.57, bf16[128,2048]{1,0:T(8,128)(2,1)} %exchange.1, f32[2048]{0:T(1024)} %bitcast.60, f32[128]{0:T(128)S(1)} %add_rsqrt_fusion), kind=kOutput, calls=%fused_computation.23 | convolution fusion | flops 1075052544 | bytes 9445888 | tf_op jit(solution)/shard_map/bld,dhe->blhe/dot_general | solution.py:180
  102.8 0.0 copy-done
  102.8 0.0 copy-done.1
  102.8 5.2 %fusion.29 = f32[16,128,128]{1,2,0:T(8,128)S(1)} fusion(bf16[128,16,128]{2,0,1:T(8,128)(2,1)S(1)} %fusion.33, bf16[2048,16,128]{2,1,0:T(8,128)(2,1)} %bitcast.58, pred[128,128]{0,1:T(8,128)(4,1)S(1)} %iota_compare_fusion, bf16[128,2048]{1,0:T(8,128)(2,1)S(1)} %copy-done, f32[2048]{0:T(1024)S(1)} %bitcast.61, f32[128]{0:T(128)S(1)} %add_rsqrt_fusion), kind=kOutput, calls=%fused_computation.20 | convolution fusion | flops 1142685696 | bytes 10510848 | tf_op jit(solution)/shard_map/bqhe,bkhe->bhqk/dot_general | solution.py:185
  108.1 0.2 fusion.54
  108.3 7.2 %fusion.30 = bf16[128,16,128]{0,2,1:T(8,128)(2,1)S(1)} fusion(bf16[2048,16,128]{2,1,0:T(8,128)(2,1)} %bitcast.59, bf16[128,2048]{1,0:T(8,128)(2,1)S(1)} %copy-done, f32[2048]{0:T(1024)S(1)} %bitcast.62, f32[128]{0:T(128)S(1)} %add_rsqrt_fusion), kind=kOutput, calls=%fused_computation.22 | convolution fusion | flops 1075052544 | bytes 9445888 | tf_op jit(solution)/shard_map/bld,dhe->blhe/dot_general | solution.py:182
  115.5 5.7 %fusion.24 = bf16[1,1,128,2048]{3,2,1,0:T(8,128)(2,1)} fusion(bf16[1,16,128,2048]{3,2,1,0:T(8,128)(2,1)} %param.19, bf16[128,2048]{1,0:T(8,128)(2,1)S(1)} %copy-done, bf16[128,16,128]{0,2,1:T(8,128)(2,1)S(1)} %fusion.30, f32[16,128]{1,0:T(8,128)S(1)} %fusion.54, f32[16,128,128]{1,2,0:T(8,128)S(1)} %fusion.29), kind=kOutput, calls=%fused_computation.14 | convolution fusion | flops 1143212160 | bytes 11018240 | tf_op jit(solution)/shard_map/crif,ife->cre/dot_general | solution.py:189
  (2 shorter events, 0.0 us)
Async XLA Ops:
  97.6 5.2 %copy-start = (bf16[128,2048]{1,0:T(8,128)(2,1)S(1)}, bf16[128,2048]{1,0:T(8,128)(2,1)}, u32[]{:S(2)}) copy-start(bf16[128,2048]{1,0:T(8,128)(2,1)} %exchange.1) | copy-start | bytes 1572868
  97.6 5.2 %copy-start.1 = (f32[1,2048]{1,0:T(1,128)S(1)}, f32[1,2048]{1,0:T(1,128)}, u32[]{:S(2)}) copy-start(f32[1,2048]{1,0:T(1,128)} %param.15) | copy-start | bytes 24580

commit v2 on v1

--- a/solution.py
+++ b/solution.py
@@ -11,7 +11,7 @@
 NORM_EPS = 1e-6
 MESH = pl.DeviceIdType.MESH
 SIDE = 4
-CHUNKS = 4
+CHUNKS = 2
 CLASSES = [c for c in itertools.product((0, 1), repeat=3) if any(c)]
 CLASS_SIZE = [3 ** (3 - sum(c)) for c in CLASSES]
 CLASS_BASE = [sum(CLASS_SIZE[:k]) for k in range(len(CLASSES))]
@@ -34,7 +34,7 @@
         return z * 16 + y * 4 + x
 
     def cube(i):
-        return (i // 9 - 1, (i // 3) % 3 - 1, i % 3 - 1)
+        return ((i + i // 9) % 3 - 1, (i + i // 3) % 3 - 1, i % 3 - 1)
 
     def free_offset(cls, i):
         out = []

time: 122 us -> 135 us (1.11)
  Pallas kernels: 94.2 us -> 108 us
    pallas_call x1, Pallas kernels: 94.2 us -> 108 us  [exchange(): pl.pallas_call(exchange_kernel, out_shape=jax.ShapeDtypeStruct((seq, d),...]
where the time goes in v2:
time: 135 us
  Pallas kernels  108 us (80%)
  matrix products  23.3 us (17%)
  other arithmetic  2.87 us (2%)
    pallas_call x1, Pallas kernels, exchange(): pl.pallas_call(exchange_kernel, out_shape=jax.ShapeDtypeStruct((seq, d),...  108 us
    dot_general x1, matrix products, attention_block(): jnp.einsum('bld,dhe->blhe', x_in, w_value, preferred_element_type=jnp.flo...  7.2 us
    dot_general x1, matrix products, attention_block(): jnp.einsum('crif,ife->cre', attn_out, w_out, preferred_element_type=jnp.f...  5.74 us
    dot_general x1, matrix products, attention_block(): jnp.einsum('bqhe,bkhe->bhqk', q_heads, k_heads, preferred_element_type=jn...  5.23 us
    dot_general x1, matrix products, attention_block(): jnp.einsum('bld,dhe->blhe', x_in, w_query, preferred_element_type=jnp.flo...  5.15 us

profile of v2, /device:TPU:1, one launch (start us, length us, event | category | flops | bytes accessed | tf_op | source)
XLA Modules:
  0.0 134.9 jit_solution(9854325944962698130)
XLA Ops:
  0.0 0.7 select_convert_fusion
  0.7 0.7 pad_maximum_fusion
  1.4 0.7 copy.21
  2.1 107.9 %exchange.1 = bf16[128,2048]{1,0:T(8,128)(2,1)} custom-call(bf16[64,24,2048]{2,1,0:T(8,128)(2,1)} %bitcast.54, f32[128,16]{1,0:T(8,128)} %bitcast.56, bf16[128,2048]{1,0:T(8,128)(2,1)} %bitcast.55), custom_call_target="tpu_custom_call" | custom-call | tf_op jit(solution)/shard_map/exchange/pallas_call | solution.py:153
  110.1 1.2 fusion.42
  111.3 0.0 copy-start
  111.3 0.0 copy-start.1
  111.4 5.2 %fusion.33 = bf16[128,16,128]{2,0,1:T(8,128)(2,1)S(1)} fusion(bf16[2048,16,128]{2,1,0:T(8,128)(2,1)} %bitcast.57, bf16[128,2048]{1,0:T(8,128)(2,1)} %exchange.1, f32[2048]{0:T(1024)} %bitcast.60, f32[128]{0:T(128)S(1)} %add_rsqrt_fusion), kind=kOutput, calls=%fused_computation.23 | convolution fusion | flops 1075052544 | bytes 9445888 | tf_op jit(solution)/shard_map/bld,dhe->blhe/dot_general | solution.py:180
  116.5 0.0 copy-done
  116.5 0.0 copy-done.1
  116.5 5.2 %fusion.29 = f32[16,128,128]{1,2,0:T(8,128)S(1)} fusion(bf16[128,16,128]{2,0,1:T(8,128)(2,1)S(1)} %fusion.33, bf16[2048,16,128]{2,1,0:T(8,128)(2,1)} %bitcast.58, pred[128,128]{0,1:T(8,128)(4,1)S(1)} %iota_compare_fusion, bf16[128,2048]{1,0:T(8,128)(2,1)S(1)} %copy-done, f32[2048]{0:T(1024)S(1)} %bitcast.61, f32[128]{0:T(128)S(1)} %add_rsqrt_fusion), kind=kOutput, calls=%fused_computation.20 | convolution fusion | flops 1142685696 | bytes 10510848 | tf_op jit(solution)/shard_map/bqhe,bkhe->bhqk/dot_general | solution.py:185
  121.8 0.2 fusion.54
  122.0 7.2 %fusion.30 = bf16[128,16,128]{0,2,1:T(8,128)(2,1)S(1)} fusion(bf16[2048,16,128]{2,1,0:T(8,128)(2,1)} %bitcast.59, bf16[128,2048]{1,0:T(8,128)(2,1)S(1)} %copy-done, f32[2048]{0:T(1024)S(1)} %bitcast.62, f32[128]{0:T(128)S(1)} %add_rsqrt_fusion), kind=kOutput, calls=%fused_computation.22 | convolution fusion | flops 1075052544 | bytes 9445888 | tf_op jit(solution)/shard_map/bld,dhe->blhe/dot_general | solution.py:182
  129.2 5.7 %fusion.24 = bf16[1,1,128,2048]{3,2,1,0:T(8,128)(2,1)} fusion(bf16[1,16,128,2048]{3,2,1,0:T(8,128)(2,1)} %param.19, bf16[128,2048]{1,0:T(8,128)(2,1)S(1)} %copy-done, bf16[128,16,128]{0,2,1:T(8,128)(2,1)S(1)} %fusion.30, f32[16,128]{1,0:T(8,128)S(1)} %fusion.54, f32[16,128,128]{1,2,0:T(8,128)S(1)} %fusion.29), kind=kOutput, calls=%fused_computation.14 | convolution fusion | flops 1143212160 | bytes 11018240 | tf_op jit(solution)/shard_map/crif,ife->cre/dot_general | solution.py:189
  (2 shorter events, 0.0 us)
Async XLA Ops:
  111.3 5.2 %copy-start = (bf16[128,2048]{1,0:T(8,128)(2,1)S(1)}, bf16[128,2048]{1,0:T(8,128)(2,1)}, u32[]{:S(2)}) copy-start(bf16[128,2048]{1,0:T(8,128)(2,1)} %exchange.1) | copy-start | bytes 1572868
  111.3 5.2 %copy-start.1 = (f32[1,2048]{1,0:T(1,128)S(1)}, f32[1,2048]{1,0:T(1,128)}, u32[]{:S(2)}) copy-start(f32[1,2048]{1,0:T(1,128)} %param.15) | copy-start | bytes 24580

commit v3 on v0

v3 whole, which is shorter than its diff:
```python
import jax
import jax.numpy as jnp
from jax import lax
from jax.experimental import pallas as pl
from jax.experimental.pallas import tpu as pltpu
from jax.sharding import PartitionSpec as P

NORM_EPS = 1e-6
MESH = pl.DeviceIdType.MESH
SIDE = 4
GROUP = 8
COLORS = 3
ORDERS = ((2, 1, 0), (1, 0, 2), (0, 2, 1))
FIRST, SECOND = (0, 3, 1, 2), (0, 3, 1, 2)


def exchange_kernel(o_ref, kg_ref, h_ref, y_ref, rows, held1, held2, tie1, tie2, tie3, kg_in, h_in, g_mat, acc, side_sem, send_sem, recv1, recv2, recv3, recv_rows):
    stage = lax.axis_index('pp')
    me = lax.axis_index('ep')
    other = 1 - stage
    pos = (me // 16, (me // 4) % 4, me % 4)
    sign = [1 - 2 * (p % 2) for p in pos]
    to_a = [lax.rem(p + s + SIDE, SIDE) for p, s in zip(pos, sign)]
    to_b = [lax.rem(p - s + SIDE, SIDE) for p, s in zip(pos, sign)]
    far = [lax.rem(p + 2, SIDE) for p in pos]
    seq = kg_in.shape[0]
    width = 512

    def rank(axis, value):
        z, y, x = [value if k == axis else p for k, p in enumerate(pos)]
        return z * 16 + y * 4 + x

    near_a = [rank(k, to_a[k]) for k in range(3)]
    near_b = [rank(k, to_b[k]) for k in range(3)]

    barrier = pltpu.get_barrier_semaphore()
    peers = [(other, me)]
    for k in range(3):
        for where in (near_a[k], near_b[k]):
            peers += [(stage, where), (other, where)]
    for peer in peers:
        pl.semaphore_signal(barrier, inc=1, device_id=peer, device_id_type=MESH)
    pl.semaphore_wait(barrier, len(peers))

    def send(src, dst, send_s, recv_s, peer):
        pltpu.make_async_remote_copy(src_ref=src, dst_ref=dst, send_sem=send_s, recv_sem=recv_s, device_id=peer, device_id_type=MESH).start()

    def wait(ref, sem):
        pltpu.make_async_copy(ref, ref, sem).wait()

    def table(c, fixed):
        return o_ref.at[tuple(fixed.get(k, slice(None)) for k in range(3)) + (c,)]

    def from_first(c, r1, fixed):
        d1 = ORDERS[c][0]
        if r1 == 0:
            return table(c, {d1: pos[d1], **fixed})
        return held1.at[(c, r1 - 1) + tuple(fixed.get(k, slice(None)) for k in range(3) if k != d1)]

    def phase1():
        for c in range(COLORS):
            d = ORDERS[c][0]
            send(table(c, {d: far[d]}), tie1.at[c], send_sem.at[0, c], recv1.at[c, 0], (stage, near_a[d]))
        for c in range(COLORS):
            d = ORDERS[c][0]
            send(table(c, {d: to_b[d]}), held1.at[c, 2], send_sem.at[0, c], recv1.at[c, 3], (stage, near_b[d]))
        for c in range(COLORS):
            d = ORDERS[c][0]
            send(table(c, {d: to_a[d]}), held1.at[c, 0], send_sem.at[0, c], recv1.at[c, 1], (stage, near_a[d]))

    def forward1():
        for c in range(COLORS):
            d = ORDERS[c][0]
            wait(tie1.at[c], recv1.at[c, 0])
            send(tie1.at[c], held1.at[c, 1], send_sem.at[0, c], recv1.at[c, 2], (stage, near_b[d]))

    def phase2(r1):
        for c in range(COLORS):
            d = ORDERS[c][1]
            if r1:
                wait(held1.at[c, r1 - 1], recv1.at[c, r1])
            send(from_first(c, r1, {d: to_b[d]}), held2.at[c, r1, 2], send_sem.at[1, c], recv2.at[c, r1, 3], (stage, near_b[d]))
            send(from_first(c, r1, {d: far[d]}), tie2.at[c, r1], send_sem.at[1, c], recv2.at[c, r1, 0], (stage, near_a[d]))
            send(from_first(c, r1, {d: to_a[d]}), held2.at[c, r1, 0], send_sem.at[1, c], recv2.at[c, r1, 1], (stage, near_a[d]))

    def forward2(r1):
        for c in range(COLORS):
            d = ORDERS[c][1]
            wait(tie2.at[c, r1], recv2.at[c, r1, 0])
            send(tie2.at[c, r1], held2.at[c, r1, 1], send_sem.at[1, c], recv2.at[c, r1, 2], (stage, near_b[d]))

    def phase3(r1):
        for c in range(COLORS):
            d2, d = ORDERS[c][1:]
            for r2 in (1, 2, 3):
                wait(held2.at[c, r1, r2 - 1], recv2.at[c, r1, r2])

            def piece(near, value):
                if near:
                    return from_first(c, r1, {d2: pos[d2], d: value})
                return held2.at[c, r1, :, value]

            for near in (True, False):
                part = 0 if near else pl.ds(1, 3)
                send(piece(near, far[d]), tie3.at[c, r1, part], send_sem.at[2, c], recv3.at[c, r1], (stage, near_a[d]))
                send(piece(near, to_b[d]), rows.at[r1, c, part, 3], send_sem.at[2, c], recv_rows.at[r1], (other, near_b[d]))
            for near in (True, False):
                part = 0 if near else pl.ds(1, 3)
                send(piece(near, to_a[d]), rows.at[r1, c, part, 1], send_sem.at[2, c], recv_rows.at[r1], (other, near_a[d]))
                send(piece(near, pos[d]), rows.at[r1, c, part, 0], send_sem.at[3, c], recv_rows.at[r1], (other, me))

    def forward3(r1):
        for c in range(COLORS):
            d = ORDERS[c][2]
            wait(tie3.at[c, r1], recv3.at[c, r1])
            send(tie3.at[c, r1], rows.at[r1, c, :, 2], send_sem.at[2, c], recv_rows.at[r1], (other, near_b[d]))

    side = [
        pltpu.make_async_remote_copy(src_ref=src, dst_ref=dst, send_sem=side_sem.at[0, k], recv_sem=side_sem.at[1, k], device_id=(other, me), device_id_type=MESH)
        for k, (src, dst) in enumerate(((kg_ref, kg_in), (h_ref, h_in)))
    ]

    def build_gates():
        for copy in side:
            copy.wait_recv()
        kg = kg_in[...]
        step = 256
        for b in range(g_mat.shape[1] // step):
            col = (lax.broadcasted_iota(jnp.int32, (seq, step), 1) + b * step).astype(jnp.float32)
            val = jnp.zeros((seq, step), jnp.float32)
            for i in range(8):
                val = jnp.where(kg[:, i:i + 1] == col, kg[:, 8 + i:9 + i], val)
            high = val.astype(jnp.bfloat16)
            rest = val - high.astype(jnp.float32)
            mid = rest.astype(jnp.bfloat16)
            low = (rest - mid.astype(jnp.float32)).astype(jnp.bfloat16)
            for part, piece in enumerate((high, mid, low)):
                g_mat[part * seq:(part + 1) * seq, b * step:(b + 1) * step] = piece
        acc[...] = h_in[...].astype(jnp.float32)

    def combine(r1):
        wait(rows.at[r1], recv_rows.at[r1])
        depth = COLORS * 16 * GROUP
        gates = g_mat[:, r1 * depth:(r1 + 1) * depth]
        for b in range(acc.shape[1] // width):
            cols = slice(b * width, (b + 1) * width)
            part = rows[r1, :, :, :, :, cols].reshape(depth, width)
            sums = jnp.dot(gates, part, preferred_element_type=jnp.float32)
            acc[:, cols] += sums[:seq] + (sums[seq:2 * seq] + sums[2 * seq:])

    phase1()
    for copy in side:
        copy.start()
    phase2(0)
    build_gates()
    forward1()
    phase2(3)
    forward2(0)
    phase2(1)
    forward2(3)
    phase2(2)
    phase3(0)
    forward2(1)
    phase3(3)
    forward2(2)
    forward3(0)
    phase3(1)
    forward3(3)
    phase3(2)
    combine(0)
    forward3(1)
    combine(3)
    forward3(2)
    combine(1)
    combine(2)
    y_ref[...] = acc[...].astype(jnp.bfloat16)

    for copy in side:
        copy.wait_send()
    for c in range(COLORS):
        for k in range(3):
            wait(rows.at[:, 0], send_sem.at[k, c])
        wait(rows.at[0, 0], send_sem.at[3, c])


def exchange(o_tab, kg, h):
    seq, d = h.shape
    dma = pltpu.SemaphoreType.DMA
    block = (GROUP, d)

    def buf(*lead):
        return pltpu.VMEM(lead + block, jnp.bfloat16)

    return pl.pallas_call(
        exchange_kernel,
        out_shape=jax.ShapeDtypeStruct((seq, d), jnp.bfloat16),
        in_specs=[pl.BlockSpec(memory_space=pl.ANY), pl.BlockSpec(memory_space=pltpu.VMEM), pl.BlockSpec(memory_space=pltpu.VMEM)],
        out_specs=pl.BlockSpec(memory_space=pltpu.VMEM),
        scratch_shapes=[
            buf(4, COLORS, 4, 4),
            buf(COLORS, 3, 4, 4),
            buf(COLORS, 4, 3, 4),
            buf(COLORS, 4, 4),
            buf(COLORS, 4, 4),
            buf(COLORS, 4, 4),
            pltpu.VMEM(kg.shape, jnp.float32),
            pltpu.VMEM((seq, d), jnp.bfloat16),
            pltpu.VMEM((3 * seq, 64 * COLORS * GROUP), jnp.bfloat16),
            pltpu.VMEM((seq, d), jnp.float32),
            dma((2, 2)),
            dma((4, COLORS)),
            dma((COLORS, 4)),
            dma((COLORS, 4, 4)),
            dma((COLORS, 4)),
            dma((4,)),
        ],
        compiler_params=pltpu.CompilerParams(collective_id=0, has_side_effects=True, vmem_limit_bytes=60 * 1024 * 1024),
        name='exchange',
    )(o_tab, kg, h)


def gate_columns(expert_ids, slot_ids, slots):
    me = lax.axis_index('ep')
    local = slot_ids - me * slots
    colour = local // GROUP
    roles = []
    for shift in (4, 2, 0):
        mine = (me >> shift) & 3
        roles.append(((1 - 2 * (mine & 1)) * (((expert_ids >> shift) & 3) - mine)) & 3)
    first, second, third = [
        jnp.where(colour == 0, roles[ORDERS[0][k]], jnp.where(colour == 1, roles[ORDERS[1][k]], roles[ORDERS[2][k]]))
        for k in range(3)
    ]
    column = (((first * COLORS + colour) * 4 + second) * 4 + third) * GROUP + local % GROUP
    return jnp.where(slot_ids >= 0, column, -1)


def attention_block(combined, norm_w, w_query, w_key, w_value, w_out):
    y_wide = combined.astype(jnp.float32)
    inv_rms = lax.rsqrt(jnp.mean(y_wide * y_wide, axis=-1, keepdims=True) + NORM_EPS)
    x_in = (y_wide * inv_rms * norm_w).astype(jnp.bfloat16)
    q_heads = jnp.einsum('bld,dhe->blhe', x_in, w_query, preferred_element_type=jnp.float32).astype(jnp.bfloat16)
    k_heads = jnp.einsum('bld,dhe->blhe', x_in, w_key, preferred_element_type=jnp.float32).astype(jnp.bfloat16)
    v_heads = jnp.einsum('bld,dhe->blhe', x_in, w_value, preferred_element_type=jnp.float32).astype(jnp.bfloat16)
    head_dim = w_query.shape[2]
    seq_len = combined.shape[1]
    scores = jnp.einsum('bqhe,bkhe->bhqk', q_heads, k_heads, preferred_element_type=jnp.float32) * (head_dim ** -0.5)
    causal = jnp.arange(seq_len)[:, None] >= jnp.arange(seq_len)[None, :]
    attn_probs = jax.nn.softmax(jnp.where(causal, scores, -jnp.inf), axis=-1).astype(jnp.bfloat16)
    attn_out = jnp.einsum('bhqk,bkhe->bqhe', attn_probs, v_heads, preferred_element_type=jnp.float32).astype(jnp.bfloat16)
    out_proj = jnp.einsum('crif,ife->cre', attn_out, w_out, preferred_element_type=jnp.float32).astype(jnp.bfloat16)
    return (y_wide + out_proj.astype(jnp.float32)).astype(jnp.bfloat16)


def solution(mesh):
    n = mesh.shape['ep']
    tok_spec = P('pp', 'ep', None, None)
    wt_spec = P('pp', None, None, None)

    def device_step(expert_out, expert_ids, slot_ids, gate_vals, residual, norm_w, w_query, w_key, w_value, w_out):
        num_micro, seqs_dev, seq_len, d_model = residual.shape
        slots = expert_out.shape[2] // n
        key = gate_columns(expert_ids, slot_ids, slots)
        kg = jnp.concatenate([key.astype(jnp.float32), gate_vals], axis=-1).reshape(seq_len, -1)
        o_tab = expert_out.reshape(SIDE, SIDE, SIDE, COLORS, GROUP, d_model)
        arrived = exchange(o_tab, kg, residual.reshape(seq_len, d_model))
        result = attention_block(arrived.reshape(1, seq_len, d_model), norm_w[0], w_query[0], w_key[0], w_value[0], w_out[0])
        return result.reshape(num_micro, seqs_dev, seq_len, d_model)

    return jax.shard_map(device_step, mesh=mesh, in_specs=(tok_spec, tok_spec, tok_spec, tok_spec, tok_spec, P('pp', None), wt_spec, wt_spec, wt_spec, wt_spec), out_specs=tok_spec, check_vma=False)
```

time: 281 us -> 109 us (0.39); the launches traced: 278 us -> 109 us
  local copies, waits for them, and re-layouts: 103 us -> 0.74 us
  waiting for transfers between devices: 90 us -> 0 us
  Pallas kernels: 0 us -> 82.1 us
  other arithmetic: 46 us -> 2.88 us
  starting transfers between devices: 17.8 us -> 0 us
    all_to_all x1 -> x0, waiting for transfers between devices: 88.5 us -> none  [device_step(): returned = lax.all_to_all(expert_out, 'ep', 2, 1, tiled=True)]
    pallas_call x0 -> x1, Pallas kernels: none -> 82.1 us  [exchange(): pl.pallas_call(exchange_kernel, out_shape=jax.ShapeDtypeStruct((seq, d),...]
    unnamed x15 -> x4, local copies, waits for them, and re-layouts: 75.9 us -> 0.01 us
    unnamed x1 -> x0, other arithmetic: 38.9 us -> none
    gather x4 -> x0, local copies, waits for them, and re-layouts: 26.9 us -> none  [gated_sum(): exp_rows[id_blk, pos_blk]]
    all_to_all x1 -> x0, starting transfers between devices: 12.5 us -> none  [device_step(): returned = lax.all_to_all(expert_out, 'ep', 2, 1, tiled=True)]
    reduce_sum x1 -> x0, other arithmetic: 6.53 us -> none  [gated_sum(): jnp.sum(weight[..., None] * picked.astype(jnp.float32), axis=3)]
    ppermute x1 -> x0, starting transfers between devices: 5.26 us -> none  [device_step(): arrived = lax.ppermute(combined, 'pp', send_next)]
  transfers between devices with their start and end apart: 2 -> 0, of which waited for: 2 -> 0; matrix products, arithmetic and copies ran while one was open for 0% -> 0% of each run, Pallas kernels for 0% -> 0%
where the time goes in v3:
time: 109 us
  Pallas kernels  82.1 us (75%)
  matrix products  23.3 us (21%)
  other arithmetic  2.88 us (3%)
    pallas_call x1, Pallas kernels, exchange(): pl.pallas_call(exchange_kernel, out_shape=jax.ShapeDtypeStruct((seq, d),...  82.1 us
    dot_general x1, matrix products, attention_block(): jnp.einsum('bld,dhe->blhe', x_in, w_value, preferred_element_type=jnp.flo...  7.2 us
    dot_general x1, matrix products, attention_block(): jnp.einsum('crif,ife->cre', attn_out, w_out, preferred_element_type=jnp.f...  5.74 us
    dot_general x1, matrix products, attention_block(): jnp.einsum('bqhe,bkhe->bhqk', q_heads, k_heads, preferred_element_type=jn...  5.23 us
    dot_general x1, matrix products, attention_block(): jnp.einsum('bld,dhe->blhe', x_in, w_query, preferred_element_type=jnp.flo...  5.15 us

profile of v3, /device:TPU:1, one launch (start us, length us, event | category | flops | bytes accessed | tf_op | source)
XLA Modules:
  0.0 109.1 jit_solution(4029563108753767141)
XLA Ops:
  0.0 0.7 fusion.54
  0.7 0.7 pad_maximum_fusion
  1.4 0.7 copy.26
  2.2 82.1 %exchange.1 = bf16[128,2048]{1,0:T(8,128)(2,1)} custom-call(bf16[4,4,4,3,8,2048]{5,4,3,2,1,0:T(8,128)(2,1)} %bitcast.54, f32[128,16]{1,0:T(8,128)} %bitcast.56, bf16[128,2048]{1,0:T(8,128)(2,1)} %bitcast.55), custom_call_target="tpu_custom_call" | custom-call | tf_op jit(solution)/shard_map/exchange/pallas_call | solution.py:194
  84.3 1.2 %fusion.42 = f32[128]{0:T(128)S(1)} fusion(bf16[128,2048]{1,0:T(8,128)(2,1)} %exchange.1), kind=kLoop, calls=%fused_computation.26 | loop fusion | flops 786304 | bytes 524800 | tf_op jit(solution)/shard_map/reduce_sum | solution.py:240
  85.5 0.0 copy-start
  85.6 0.0 copy-start.1
  85.6 5.2 %fusion.33 = bf16[128,16,128]{2,0,1:T(8,128)(2,1)S(1)} fusion(bf16[2048,16,128]{2,1,0:T(8,128)(2,1)} %bitcast.57, bf16[128,2048]{1,0:T(8,128)(2,1)} %exchange.1, f32[2048]{0:T(1024)} %bitcast.60, f32[128]{0:T(128)S(1)} %add_rsqrt_fusion), kind=kOutput, calls=%fused_computation.23 | convolution fusion | flops 1075052544 | bytes 9445888 | tf_op jit(solution)/shard_map/bld,dhe->blhe/dot_general | solution.py:242
  90.7 0.0 copy-done
  90.7 0.0 copy-done.1
  90.7 5.2 %fusion.29 = f32[16,128,128]{1,2,0:T(8,128)S(1)} fusion(bf16[128,16,128]{2,0,1:T(8,128)(2,1)S(1)} %fusion.33, bf16[2048,16,128]{2,1,0:T(8,128)(2,1)} %bitcast.58, pred[128,128]{0,1:T(8,128)(4,1)S(1)} %iota_compare_fusion, bf16[128,2048]{1,0:T(8,128)(2,1)S(1)} %copy-done, f32[2048]{0:T(1024)S(1)} %bitcast.61, f32[128]{0:T(128)S(1)} %add_rsqrt_fusion), kind=kOutput, calls=%fused_computation.20 | convolution fusion | flops 1142685696 | bytes 10510848 | tf_op jit(solution)/shard_map/bqhe,bkhe->bhqk/dot_general | solution.py:247
  96.0 0.2 fusion.61
  96.2 7.2 %fusion.30 = bf16[128,16,128]{0,2,1:T(8,128)(2,1)S(1)} fusion(bf16[2048,16,128]{2,1,0:T(8,128)(2,1)} %bitcast.59, bf16[128,2048]{1,0:T(8,128)(2,1)S(1)} %copy-done, f32[2048]{0:T(1024)S(1)} %bitcast.62, f32[128]{0:T(128)S(1)} %add_rsqrt_fusion), kind=kOutput, calls=%fused_computation.22 | convolution fusion | flops 1075052544 | bytes 9445888 | tf_op jit(solution)/shard_map/bld,dhe->blhe/dot_general | solution.py:244
  103.4 5.7 %fusion.24 = bf16[1,1,128,2048]{3,2,1,0:T(8,128)(2,1)} fusion(bf16[1,16,128,2048]{3,2,1,0:T(8,128)(2,1)} %param.19, bf16[128,2048]{1,0:T(8,128)(2,1)S(1)} %copy-done, bf16[128,16,128]{0,2,1:T(8,128)(2,1)S(1)} %fusion.30, f32[16,128]{1,0:T(8,128)S(1)} %fusion.61, f32[16,128,128]{1,2,0:T(8,128)S(1)} %fusion.29), kind=kOutput, calls=%fused_computation.14 | convolution fusion | flops 1143212160 | bytes 11018240 | tf_op jit(solution)/shard_map/crif,ife->cre/dot_general | solution.py:251
  (2 shorter events, 0.0 us)
Async XLA Ops:
  85.5 5.2 %copy-start = (bf16[128,2048]{1,0:T(8,128)(2,1)S(1)}, bf16[128,2048]{1,0:T(8,128)(2,1)}, u32[]{:S(2)}) copy-start(bf16[128,2048]{1,0:T(8,128)(2,1)} %exchange.1) | copy-start | bytes 1572868
  85.6 5.2 %copy-start.1 = (f32[1,2048]{1,0:T(1,128)S(1)}, f32[1,2048]{1,0:T(1,128)}, u32[]{:S(2)}) copy-start(f32[1,2048]{1,0:T(1,128)} %param.15) | copy-start | bytes 24580

commit v4 on v3

--- a/solution.py
+++ b/solution.py
@@ -14,7 +14,7 @@
 FIRST, SECOND = (0, 3, 1, 2), (0, 3, 1, 2)
 
 
-def exchange_kernel(o_ref, kg_ref, h_ref, y_ref, rows, held1, held2, tie1, tie2, tie3, kg_in, h_in, g_mat, acc, side_sem, send_sem, recv1, recv2, recv3, recv_rows):
+def stage_kernel(o_ref, ids_ref, slots_ref, gates_ref, h_ref, norm_ref, wq_ref, wk_ref, wv_ref, wo_ref, z_ref, rows, held1, held2, tie1, tie2, tie3, ids_in, slots_in, gates_in, h_in, g_mat, acc, norm_in, flat, wo_in, raw, x_in, a_in, side_sem, local_sem, raw_sem, send_sem, recv1, recv2, recv3, recv_rows):
     stage = lax.axis_index('pp')
     me = lax.axis_index('ep')
     other = 1 - stage
@@ -23,8 +23,10 @@
     to_a = [lax.rem(p + s + SIDE, SIDE) for p, s in zip(pos, sign)]
     to_b = [lax.rem(p - s + SIDE, SIDE) for p, s in zip(pos, sign)]
     far = [lax.rem(p + 2, SIDE) for p in pos]
-    seq = kg_in.shape[0]
+    seq, d_model = h_in.shape
     width = 512
+    piece_rows = raw.shape[1]
+    pieces = flat.shape[1] // piece_rows
 
     def rank(axis, value):
         z, y, x = [value if k == axis else p for k, p in enumerate(pos)]
@@ -117,19 +119,49 @@
 
     side = [
         pltpu.make_async_remote_copy(src_ref=src, dst_ref=dst, send_sem=side_sem.at[0, k], recv_sem=side_sem.at[1, k], device_id=(other, me), device_id_type=MESH)
-        for k, (src, dst) in enumerate(((kg_ref, kg_in), (h_ref, h_in)))
+        for k, (src, dst) in enumerate(((ids_ref, ids_in), (slots_ref, slots_in), (gates_ref, gates_in), (h_ref, h_in)))
     ]
+    local = [pltpu.make_async_copy(src, dst, local_sem.at[k]) for k, (src, dst) in enumerate(((norm_ref, norm_in), (wo_ref, wo_in)))]
+
+    def load(i):
+        src = (wq_ref, wk_ref, wv_ref)[i // pieces]
+        return pltpu.make_async_copy(src.at[pl.ds(i % pieces * piece_rows, piece_rows)], raw.at[i % 2], raw_sem.at[i % 2])
+
+    def flatten(i):
+        load(i).wait()
+        step = 64
+
+        def body(j, carry):
+            at = pl.multiple_of(j * step, step)
+            flat[i // pieces, pl.ds(pl.multiple_of(i % pieces * piece_rows + at, step), step), :] = raw[i % 2, pl.ds(at, step)].reshape(step, d_model)
+            return carry
+
+        lax.fori_loop(0, piece_rows // step, body, 0)
+        if i + 2 < 3 * pieces:
+            load(i + 2).start()
 
     def build_gates():
         for copy in side:
             copy.wait_recv()
-        kg = kg_in[...]
+        ids, slot = ids_in[...], slots_in[...]
+        spot = slot - me * (COLORS * GROUP)
+        colour = spot >> 3
+        roles = []
+        for k, shift in enumerate((4, 2, 0)):
+            roles.append((sign[k] * (((ids >> shift) & 3) - pos[k])) & 3)
+        first, second, third = [
+            jnp.where(colour == 0, roles[ORDERS[0][k]], jnp.where(colour == 1, roles[ORDERS[1][k]], roles[ORDERS[2][k]]))
+            for k in range(3)
+        ]
+        column = (((first * COLORS + colour) * 4 + second) * 4 + third) * GROUP + (spot & 7)
+        column = jnp.where(slot >= 0, column, -1).astype(jnp.float32)
+        both = jnp.concatenate([column, gates_in[...], jnp.zeros((112, seq), jnp.float32)], axis=0).T
         step = 256
         for b in range(g_mat.shape[1] // step):
             col = (lax.broadcasted_iota(jnp.int32, (seq, step), 1) + b * step).astype(jnp.float32)
             val = jnp.zeros((seq, step), jnp.float32)
             for i in range(8):
-                val = jnp.where(kg[:, i:i + 1] == col, kg[:, 8 + i:9 + i], val)
+                val = jnp.where(both[:, i:i + 1] == col, both[:, 8 + i:9 + i], val)
             high = val.astype(jnp.bfloat16)
             rest = val - high.astype(jnp.float32)
             mid = rest.astype(jnp.bfloat16)
@@ -148,18 +180,62 @@
             sums = jnp.dot(gates, part, preferred_element_type=jnp.float32)
             acc[:, cols] += sums[:seq] + (sums[seq:2 * seq] + sums[2 * seq:])
 
+    def norm():
+        total = jnp.zeros((seq, 1), jnp.float32)
+        for b in range(d_model // width):
+            cols = slice(b * width, (b + 1) * width)
+            y = acc[:, cols].astype(jnp.bfloat16).astype(jnp.float32)
+            acc[:, cols] = y
+            total += jnp.sum(y * y, axis=1, keepdims=True)
+        inv = lax.rsqrt(total * (1.0 / d_model) + NORM_EPS)
+        for b in range(d_model // width):
+            cols = slice(b * width, (b + 1) * width)
+            x_in[:, cols] = (acc[:, cols] * inv * norm_in[:, cols]).astype(jnp.bfloat16)
+
+    head = 128
+    pair = 2 * head
+
+    def project(p):
+        cols = slice(p * pair, (p + 1) * pair)
+        return [jnp.dot(x_in[...], flat[k, :, cols], preferred_element_type=jnp.float32).astype(jnp.bfloat16) for k in range(3)]
+
+    causal = lax.broadcasted_iota(jnp.int32, (seq, seq), 0) >= lax.broadcasted_iota(jnp.int32, (seq, seq), 1)
+
+    def attend(p, qkv):
+        for u in range(2):
+            q, k, v = [t[:, u * head:(u + 1) * head] for t in qkv]
+            scores = lax.dot_general(q, k, (((1,), (1,)), ((), ())), preferred_element_type=jnp.float32) * (head ** -0.5)
+            scores = jnp.where(causal, scores, -jnp.inf)
+            grown = jnp.exp(scores - jnp.max(scores, axis=1, keepdims=True))
+            probs = (grown * (1.0 / jnp.sum(grown, axis=1, keepdims=True))).astype(jnp.bfloat16)
+            mixed = jnp.dot(probs, v, preferred_element_type=jnp.float32).astype(jnp.bfloat16)
+            at = p * pair + u * head
+            a_in[:, at:at + head] = mixed
+
     phase1()
     for copy in side:
         copy.start()
     phase2(0)
+    load(0).start()
+    load(1).start()
+    for copy in local:
+        copy.start()
     build_gates()
+    for i in range(12):
+        flatten(i)
     forward1()
     phase2(3)
+    for i in range(12, 16):
+        flatten(i)
     forward2(0)
     phase2(1)
+    for i in range(16, 20):
+        flatten(i)
     forward2(3)
     phase2(2)
     phase3(0)
+    for i in range(20, 24):
+        flatten(i)
     forward2(1)
     phase3(3)
     forward2(2)
@@ -172,8 +248,20 @@
     combine(3)
     forward3(2)
     combine(1)
+    for copy in local:
+        copy.wait()
     combine(2)
-    y_ref[...] = acc[...].astype(jnp.bfloat16)
+    norm()
+    pairs = d_model // pair
+    ready = project(0)
+    for p in range(pairs):
+        later = project(p + 1) if p + 1 < pairs else None
+        attend(p, ready)
+        ready = later
+    for b in range(d_model // pair):
+        cols = slice(b * pair, (b + 1) * pair)
+        out = jnp.dot(a_in[...], wo_in[:, cols], preferred_element_type=jnp.float32).astype(jnp.bfloat16)
+        z_ref[:, cols] = (acc[:, cols] + out.astype(jnp.float32)).astype(jnp.bfloat16)
 
     for copy in side:
         copy.wait_send()
@@ -183,18 +271,19 @@
         wait(rows.at[0, 0], send_sem.at[3, c])
 
 
-def exchange(o_tab, kg, h):
+def run_stage(o_tab, ids, slots, gates, h, norm_w, wq, wk, wv, wo):
     seq, d = h.shape
     dma = pltpu.SemaphoreType.DMA
     block = (GROUP, d)
+    piece = 256
 
     def buf(*lead):
         return pltpu.VMEM(lead + block, jnp.bfloat16)
 
     return pl.pallas_call(
-        exchange_kernel,
+        stage_kernel,
         out_shape=jax.ShapeDtypeStruct((seq, d), jnp.bfloat16),
-        in_specs=[pl.BlockSpec(memory_space=pl.ANY), pl.BlockSpec(memory_space=pltpu.VMEM), pl.BlockSpec(memory_space=pltpu.VMEM)],
+        in_specs=[pl.BlockSpec(memory_space=pl.ANY)] * 10,
         out_specs=pl.BlockSpec(memory_space=pltpu.VMEM),
         scratch_shapes=[
             buf(4, COLORS, 4, 4),
@@ -203,68 +292,47 @@
             buf(COLORS, 4, 4),
             buf(COLORS, 4, 4),
             buf(COLORS, 4, 4),
-            pltpu.VMEM(kg.shape, jnp.float32),
+            pltpu.VMEM(ids.shape, jnp.int32),
+            pltpu.VMEM(slots.shape, jnp.int32),
+            pltpu.VMEM(gates.shape, jnp.float32),
             pltpu.VMEM((seq, d), jnp.bfloat16),
             pltpu.VMEM((3 * seq, 64 * COLORS * GROUP), jnp.bfloat16),
             pltpu.VMEM((seq, d), jnp.float32),
-            dma((2, 2)),
+            pltpu.VMEM(norm_w.shape, jnp.float32),
+            pltpu.VMEM((3, d, d), jnp.bfloat16),
+            pltpu.VMEM((d, d), jnp.bfloat16),
+            pltpu.VMEM((2, piece) + wq.shape[1:], jnp.bfloat16),
+            pltpu.VMEM((seq, d), jnp.bfloat16),
+            pltpu.VMEM((seq, d), jnp.bfloat16),
+            dma((2, 4)),
+            dma((2,)),
+            dma((2,)),
             dma((4, COLORS)),
             dma((COLORS, 4)),
             dma((COLORS, 4, 4)),
             dma((COLORS, 4)),
             dma((4,)),
         ],
-        compiler_params=pltpu.CompilerParams(collective_id=0, has_side_effects=True, vmem_limit_bytes=60 * 1024 * 1024),
-        name='exchange',
-    )(o_tab, kg, h)
-
-
-def gate_columns(expert_ids, slot_ids, slots):
-    me = lax.axis_index('ep')
-    local = slot_ids - me * slots
-    colour = local // GROUP
-    roles = []
-    for shift in (4, 2, 0):
-        mine = (me >> shift) & 3
-        roles.append(((1 - 2 * (mine & 1)) * (((expert_ids >> shift) & 3) - mine)) & 3)
-    first, second, third = [
-        jnp.where(colour == 0, roles[ORDERS[0][k]], jnp.where(colour == 1, roles[ORDERS[1][k]], roles[ORDERS[2][k]]))
-        for k in range(3)
-    ]
-    column = (((first * COLORS + colour) * 4 + second) * 4 + third) * GROUP + local % GROUP
-    return jnp.where(slot_ids >= 0, column, -1)
-
-
-def attention_block(combined, norm_w, w_query, w_key, w_value, w_out):
-    y_wide = combined.astype(jnp.float32)
-    inv_rms = lax.rsqrt(jnp.mean(y_wide * y_wide, axis=-1, keepdims=True) + NORM_EPS)
-    x_in = (y_wide * inv_rms * norm_w).astype(jnp.bfloat16)
-    q_heads = jnp.einsum('bld,dhe->blhe', x_in, w_query, preferred_element_type=jnp.float32).astype(jnp.bfloat16)
-    k_heads = jnp.einsum('bld,dhe->blhe', x_in, w_key, preferred_element_type=jnp.float32).astype(jnp.bfloat16)
-    v_heads = jnp.einsum('bld,dhe->blhe', x_in, w_value, preferred_element_type=jnp.float32).astype(jnp.bfloat16)
-    head_dim = w_query.shape[2]
-    seq_len = combined.shape[1]
-    scores = jnp.einsum('bqhe,bkhe->bhqk', q_heads, k_heads, preferred_element_type=jnp.float32) * (head_dim ** -0.5)
-    causal = jnp.arange(seq_len)[:, None] >= jnp.arange(seq_len)[None, :]
-    attn_probs = jax.nn.softmax(jnp.where(causal, scores, -jnp.inf), axis=-1).astype(jnp.bfloat16)
-    attn_out = jnp.einsum('bhqk,bkhe->bqhe', attn_probs, v_heads, preferred_element_type=jnp.float32).astype(jnp.bfloat16)
-    out_proj = jnp.einsum('crif,ife->cre', attn_out, w_out, preferred_element_type=jnp.float32).astype(jnp.bfloat16)
-    return (y_wide + out_proj.astype(jnp.float32)).astype(jnp.bfloat16)
+        compiler_params=pltpu.CompilerParams(collective_id=0, has_side_effects=True, vmem_limit_bytes=67043328),
+        name='stage',
+    )(o_tab, ids, slots, gates, h, norm_w, wq, wk, wv, wo)
 
 
 def solution(mesh):
-    n = mesh.shape['ep']
     tok_spec = P('pp', 'ep', None, None)
     wt_spec = P('pp', None, None, None)
 
     def device_step(expert_out, expert_ids, slot_ids, gate_vals, residual, norm_w, w_query, w_key, w_value, w_out):
-        num_micro, seqs_dev, seq_len, d_model = residual.shape
-        slots = expert_out.shape[2] // n
-        key = gate_columns(expert_ids, slot_ids, slots)
-        kg = jnp.concatenate([key.astype(jnp.float32), gate_vals], axis=-1).reshape(seq_len, -1)
-        o_tab = expert_out.reshape(SIDE, SIDE, SIDE, COLORS, GROUP, d_model)
-        arrived = exchange(o_tab, kg, residual.reshape(seq_len, d_model))
-        result = attention_block(arrived.reshape(1, seq_len, d_model), norm_w[0], w_query[0], w_key[0], w_value[0], w_out[0])
-        return result.reshape(num_micro, seqs_dev, seq_len, d_model)
+        seq_len, d_model = residual.shape[2:]
+
+        def choices(array):
+            return array.reshape(seq_len, array.shape[3]).T
+
+        result = run_stage(
+            expert_out.reshape(SIDE, SIDE, SIDE, COLORS, GROUP, d_model),
+            choices(expert_ids), choices(slot_ids), choices(gate_vals),
+            residual.reshape(seq_len, d_model), norm_w, w_query[0], w_key[0], w_value[0], w_out[0].reshape(-1, d_model),
+        )
+        return result.reshape(residual.shape)
 
     return jax.shard_map(device_step, mesh=mesh, in_specs=(tok_spec, tok_spec, tok_spec, tok_spec, tok_spec, P('pp', None), wt_spec, wt_spec, wt_spec, wt_spec), out_specs=tok_spec, check_vma=False)

time: 109 us -> 90.9 us (0.83)
  matrix products: 23.3 us -> 0 us
  Pallas kernels: 82.1 us -> 88.6 us
  other arithmetic: 2.88 us -> 0 us
  local copies, waits for them, and re-layouts: 0.74 us -> 1.88 us
    dot_general x4 -> x0, matrix products: 23.3 us -> none  [the longest x1 7.2 us: attention_block(): jnp.einsum('bld,dhe->blhe', x_in, w_value, preferred_element_type=jnp.flo...]
    pallas_call x1, Pallas kernels: 82.1 us -> 88.6 us  [run_stage(): pl.pallas_call(stage_kernel, out_shape=jax.ShapeDtypeStruct((seq, d), jnp...]
    unnamed x4 -> x1, local copies, waits for them, and re-layouts: 0.01 us -> 1.88 us
    reduce_sum x1 -> x0, other arithmetic: 1.23 us -> none  [attention_block(): jnp.mean(y_wide * y_wide, axis=-1, keepdims=True) + NORM_EPS]
where the time goes in v4:
time: 90.9 us; the launch traced here: 90.5 us
  Pallas kernels  88.6 us (97%)
  local copies, waits for them, and re-layouts  1.88 us (2%)
    pallas_call x1, Pallas kernels, run_stage(): pl.pallas_call(stage_kernel, out_shape=jax.ShapeDtypeStruct((seq, d), jnp...  88.6 us
    unnamed x1, local copies, waits for them, and re-layouts  1.88 us

profile of v4, /device:TPU:1, one launch (start us, length us, event | category | flops | bytes accessed | tf_op | source)
XLA Modules:
  0.0 90.5 jit_solution(1239260769154339283)
XLA Ops:
  0.0 88.6 %stage.1 = bf16[128,2048]{1,0:T(8,128)(2,1)} custom-call(bf16[4,4,4,3,8,2048]{5,4,3,2,1,0:T(8,128)(2,1)} %bitcast.20, s32[8,128]{1,0:T(8,128)} %bitcast.23, s32[8,128]{1,0:T(8,128)} %bitcast.24, f32[8,128]{1,0:T(8,128)} %bitcast.25, bf16[128,2048]{1,0:T(8,128)(2,1)} %bitcast.22, f32[1,2048]{1,0:T(1,128)} %norm_ref.1, bf16[2048,16,128]{2,1,0:T(8,128)(2,1)} %bitcast.16, ...), custom_call_target="tpu_custom_call" | custom-call | tf_op jit(solution)/shard_map/stage/pallas_call | solution.py:283
  88.6 1.9 %copy.12 = bf16[1,1,128,2048]{3,2,1,0:T(8,128)(2,1)} copy(bf16[1,1,128,2048]{3,2,1,0:T(8,128)(2,1)} %bitcast.21) | data formatting | bytes 1048576

commit v5 on v4

--- a/solution.py
+++ b/solution.py
@@ -14,7 +14,7 @@
 FIRST, SECOND = (0, 3, 1, 2), (0, 3, 1, 2)
 
 
-def stage_kernel(o_ref, ids_ref, slots_ref, gates_ref, h_ref, norm_ref, wq_ref, wk_ref, wv_ref, wo_ref, z_ref, rows, held1, held2, tie1, tie2, tie3, ids_in, slots_in, gates_in, h_in, g_mat, acc, norm_in, flat, wo_in, raw, x_in, a_in, side_sem, local_sem, raw_sem, send_sem, recv1, recv2, recv3, recv_rows):
+def stage_kernel(o_ref, ids_ref, slots_ref, gates_ref, h_ref, norm_ref, wq_ref, wk_ref, wv_ref, wo_ref, z_ref, rows, held1, held2, tie1, tie2, tie3, ids_in, slots_in, gates_in, h_in, g_mat, acc, norm_in, flat, wo_in, raw, x_in, qkv, score, prob, side_sem, local_sem, raw_sem, send_sem, recv1, recv2, recv3, recv_rows):
     stage = lax.axis_index('pp')
     me = lax.axis_index('ep')
     other = 1 - stage
@@ -91,25 +91,31 @@
             wait(tie2.at[c, r1], recv2.at[c, r1, 0])
             send(tie2.at[c, r1], held2.at[c, r1, 1], send_sem.at[1, c], recv2.at[c, r1, 2], (stage, near_b[d]))
 
-    def phase3(r1):
-        for c in range(COLORS):
-            d2, d = ORDERS[c][1:]
+    def last(c, r1, value):
+        d2, d = ORDERS[c][1:]
+        return (0, from_first(c, r1, {d2: pos[d2], d: value})), (pl.ds(1, 3), held2.at[c, r1, :, value])
+
+    def ties3(r1):
+        for c in range(COLORS):
+            d = ORDERS[c][2]
             for r2 in (1, 2, 3):
                 wait(held2.at[c, r1, r2 - 1], recv2.at[c, r1, r2])
-
-            def piece(near, value):
-                if near:
-                    return from_first(c, r1, {d2: pos[d2], d: value})
-                return held2.at[c, r1, :, value]
-
-            for near in (True, False):
-                part = 0 if near else pl.ds(1, 3)
-                send(piece(near, far[d]), tie3.at[c, r1, part], send_sem.at[2, c], recv3.at[c, r1], (stage, near_a[d]))
-                send(piece(near, to_b[d]), rows.at[r1, c, part, 3], send_sem.at[2, c], recv_rows.at[r1], (other, near_b[d]))
-            for near in (True, False):
-                part = 0 if near else pl.ds(1, 3)
-                send(piece(near, to_a[d]), rows.at[r1, c, part, 1], send_sem.at[2, c], recv_rows.at[r1], (other, near_a[d]))
-                send(piece(near, pos[d]), rows.at[r1, c, part, 0], send_sem.at[3, c], recv_rows.at[r1], (other, me))
+            for part, piece in last(c, r1, far[d]):
+                send(piece, tie3.at[c, r1, part], send_sem.at[2, c], recv3.at[c, r1], (stage, near_a[d]))
+
+    def to_b3(r1):
+        for c in range(COLORS):
+            d = ORDERS[c][2]
+            for part, piece in last(c, r1, to_b[d]):
+                send(piece, rows.at[r1, c, part, 3], send_sem.at[2, c], recv_rows.at[r1], (other, near_b[d]))
+
+    def to_a3(r1):
+        for c in range(COLORS):
+            d = ORDERS[c][2]
+            for part, piece in last(c, r1, to_a[d]):
+                send(piece, rows.at[r1, c, part, 1], send_sem.at[2, c], recv_rows.at[r1], (other, near_a[d]))
+            for part, piece in last(c, r1, pos[d]):
+                send(piece, rows.at[r1, c, part, 0], send_sem.at[3, c], recv_rows.at[r1], (other, me))
 
     def forward3(r1):
         for c in range(COLORS):
@@ -194,23 +200,32 @@
 
     head = 128
     pair = 2 * head
-
-    def project(p):
+    causal = lax.broadcasted_iota(jnp.int32, (seq, seq), 0) >= lax.broadcasted_iota(jnp.int32, (seq, seq), 1)
+
+    def project(k, p):
         cols = slice(p * pair, (p + 1) * pair)
-        return [jnp.dot(x_in[...], flat[k, :, cols], preferred_element_type=jnp.float32).astype(jnp.bfloat16) for k in range(3)]
-
-    causal = lax.broadcasted_iota(jnp.int32, (seq, seq), 0) >= lax.broadcasted_iota(jnp.int32, (seq, seq), 1)
-
-    def attend(p, qkv):
-        for u in range(2):
-            q, k, v = [t[:, u * head:(u + 1) * head] for t in qkv]
-            scores = lax.dot_general(q, k, (((1,), (1,)), ((), ())), preferred_element_type=jnp.float32) * (head ** -0.5)
-            scores = jnp.where(causal, scores, -jnp.inf)
-            grown = jnp.exp(scores - jnp.max(scores, axis=1, keepdims=True))
-            probs = (grown * (1.0 / jnp.sum(grown, axis=1, keepdims=True))).astype(jnp.bfloat16)
-            mixed = jnp.dot(probs, v, preferred_element_type=jnp.float32).astype(jnp.bfloat16)
-            at = p * pair + u * head
-            a_in[:, at:at + head] = mixed
+        qkv[k, :, cols] = jnp.dot(x_in[...], flat[k, :, cols], preferred_element_type=jnp.float32).astype(jnp.bfloat16)
+
+    def softmax(h):
+        scores = jnp.where(causal, score[h] * (head ** -0.5), -jnp.inf)
+        grown = jnp.exp(scores - jnp.max(scores, axis=1, keepdims=True))
+        prob[h] = (grown * (1.0 / jnp.sum(grown, axis=1, keepdims=True))).astype(jnp.bfloat16)
+
+    def attend():
+        heads = d_model // head
+        for k in range(2):
+            for p in range(d_model // pair):
+                project(k, p)
+        for h in range(heads):
+            q, k = [qkv[t, :, h * head:(h + 1) * head] for t in range(2)]
+            score[h] = lax.dot_general(q, k, (((1,), (1,)), ((), ())), preferred_element_type=jnp.float32)
+        for p in range(d_model // pair):
+            softmax(2 * p)
+            softmax(2 * p + 1)
+            project(2, p)
+        for h in range(heads):
+            cols = slice(h * head, (h + 1) * head)
+            x_in[:, cols] = jnp.dot(prob[h], qkv[2, :, cols], preferred_element_type=jnp.float32).astype(jnp.bfloat16)
 
     phase1()
     for copy in side:
@@ -233,34 +248,37 @@
         flatten(i)
     forward2(3)
     phase2(2)
-    phase3(0)
+    ties3(0)
+    to_b3(0)
+    to_a3(0)
     for i in range(20, 24):
         flatten(i)
     forward2(1)
-    phase3(3)
+    ties3(3)
+    to_b3(3)
     forward2(2)
     forward3(0)
-    phase3(1)
+    to_a3(3)
+    ties3(1)
+    to_b3(1)
     forward3(3)
-    phase3(2)
+    ties3(2)
+    to_b3(2)
+    to_a3(1)
     combine(0)
     forward3(1)
+    to_a3(2)
     combine(3)
+    for copy in local:
+        copy.wait()
     forward3(2)
     combine(1)
-    for copy in local:
-        copy.wait()
     combine(2)
     norm()
-    pairs = d_model // pair
-    ready = project(0)
-    for p in range(pairs):
-        later = project(p + 1) if p + 1 < pairs else None
-        attend(p, ready)
-        ready = later
+    attend()
     for b in range(d_model // pair):
         cols = slice(b * pair, (b + 1) * pair)
-        out = jnp.dot(a_in[...], wo_in[:, cols], preferred_element_type=jnp.float32).astype(jnp.bfloat16)
+        out = jnp.dot(x_in[...], wo_in[:, cols], preferred_element_type=jnp.float32).astype(jnp.bfloat16)
         z_ref[:, cols] = (acc[:, cols] + out.astype(jnp.float32)).astype(jnp.bfloat16)
 
     for copy in side:
@@ -282,7 +300,7 @@
 
     return pl.pallas_call(
         stage_kernel,
-        out_shape=jax.ShapeDtypeStruct((seq, d), jnp.bfloat16),
+        out_shape=pltpu.VMEM((seq, d), jnp.bfloat16),
         in_specs=[pl.BlockSpec(memory_space=pl.ANY)] * 10,
         out_specs=pl.BlockSpec(memory_space=pltpu.VMEM),
         scratch_shapes=[
@@ -303,7 +321,9 @@
             pltpu.VMEM((d, d), jnp.bfloat16),
             pltpu.VMEM((2, piece) + wq.shape[1:], jnp.bfloat16),
             pltpu.VMEM((seq, d), jnp.bfloat16),
-            pltpu.VMEM((seq, d), jnp.bfloat16),
+            pltpu.VMEM((3, seq, d), jnp.bfloat16),
+            pltpu.VMEM((wq.shape[1], seq, seq), jnp.float32),
+            pltpu.VMEM((wq.shape[1], seq, seq), jnp.bfloat16),
             dma((2, 4)),
             dma((2,)),
             dma((2,)),
@@ -313,7 +333,7 @@
             dma((COLORS, 4)),
             dma((4,)),
         ],
-        compiler_params=pltpu.CompilerParams(collective_id=0, has_side_effects=True, vmem_limit_bytes=67043328),
+        compiler_params=pltpu.CompilerParams(collective_id=0, has_side_effects=True, vmem_limit_bytes=62 * 1024 * 1024),
         name='stage',
     )(o_tab, ids, slots, gates, h, norm_w, wq, wk, wv, wo)
 

time: 90.9 us -> 84.6 us (0.931)
  Pallas kernels: 88.6 us -> 83.5 us
  local copies, waits for them, and re-layouts: 1.88 us -> 0.8 us
    pallas_call x1, Pallas kernels: 88.6 us -> 83.5 us  [run_stage(): pl.pallas_call(stage_kernel, out_shape=pltpu.VMEM((seq, d), jnp.bfloat16)...]
    unnamed x1, local copies, waits for them, and re-layouts: 1.88 us -> 0.8 us
where the time goes in v5:
time: 84.6 us; the launch traced here: 84.3 us
  Pallas kernels  83.5 us (99%)
    pallas_call x1, Pallas kernels, run_stage(): pl.pallas_call(stage_kernel, out_shape=pltpu.VMEM((seq, d), jnp.bfloat16)...  83.5 us

profile of v5, /device:TPU:1, one launch (start us, length us, event | category | flops | bytes accessed | tf_op | source)
XLA Modules:
  0.0 84.3 jit_solution(302284941897908007)
XLA Ops:
  0.0 83.5 %stage.1 = bf16[128,2048]{1,0:T(8,128)(2,1)S(1)} custom-call(bf16[4,4,4,3,8,2048]{5,4,3,2,1,0:T(8,128)(2,1)} %bitcast.21, s32[8,128]{1,0:T(8,128)} %bitcast.23, s32[8,128]{1,0:T(8,128)} %bitcast.24, f32[8,128]{1,0:T(8,128)} %bitcast.25, bf16[128,2048]{1,0:T(8,128)(2,1)} %bitcast.22, f32[1,2048]{1,0:T(1,128)} %norm_ref.1, bf16[2048,16,128]{2,1,0:T(8,128)(2,1)} %bitcast.17, ...), custom_call_target="tpu_custom_call" | custom-call | tf_op jit(solution)/shard_map/stage/pallas_call | solution.py:301
  83.5 0.8 copy.12

commit v6 on v5

v6 whole, which is shorter than its diff:
```python
import jax
import jax.numpy as jnp
from jax import lax
from jax.experimental import pallas as pl
from jax.experimental.pallas import tpu as pltpu
from jax.sharding import PartitionSpec as P

NORM_EPS = 1e-6
MESH = pl.DeviceIdType.MESH
SIDE = 4
GROUP = 8
COLORS = 3
ORDERS = ((2, 1, 0), (1, 0, 2), (0, 2, 1))
WIDE, NARROW = 1536, 512


def stage_kernel(o_ref, ids_ref, slots_ref, gates_ref, h_ref, norm_ref, wq_ref, wk_ref, wv_ref, wo_ref, z_ref, wide, narrow, held1, held2, tie1, tie2, tie3, ids_in, slots_in, gates_in, g_wide, g_narrow, acc, norm_in, flat, wo_in, raw, x_in, part, qkv, side_sem, local_sem, raw_sem, send_sem, recv1, recv2, recv3_wide, recv3_narrow, recv_wide, recv_narrow):
    stage = lax.axis_index('pp')
    me = lax.axis_index('ep')
    other = 1 - stage
    pos = (me // 16, (me // 4) % 4, me % 4)
    sign = [1 - 2 * (p % 2) for p in pos]
    to_a = [lax.rem(p + s + SIDE, SIDE) for p, s in zip(pos, sign)]
    to_b = [lax.rem(p - s + SIDE, SIDE) for p, s in zip(pos, sign)]
    far = [lax.rem(p + 2, SIDE) for p in pos]
    seq, d_model = x_in.shape
    width = 512
    depth, piece_rows = raw.shape[:2]
    pieces = flat.shape[1] // piece_rows

    def rank(axis, value):
        z, y, x = [value if k == axis else p for k, p in enumerate(pos)]
        return z * 16 + y * 4 + x

    near_a = [rank(k, to_a[k]) for k in range(3)]
    near_b = [rank(k, to_b[k]) for k in range(3)]

    barrier = pltpu.get_barrier_semaphore()
    peers = [(other, me)]
    for k in range(3):
        for where in (near_a[k], near_b[k]):
            peers += [(stage, where), (other, where)]
    for peer in peers:
        pl.semaphore_signal(barrier, inc=1, device_id=peer, device_id_type=MESH)
    pl.semaphore_wait(barrier, len(peers))

    def send(src, dst, send_s, recv_s, peer):
        pltpu.make_async_remote_copy(src_ref=src, dst_ref=dst, send_sem=send_s, recv_sem=recv_s, device_id=peer, device_id_type=MESH).start()

    def wait(ref, sem):
        pltpu.make_async_copy(ref, ref, sem).wait()

    def table(c, fixed):
        return o_ref.at[tuple(fixed.get(k, slice(None)) for k in range(3)) + (c,)]

    def from_first(c, r1, fixed):
        d1 = ORDERS[c][0]
        if r1 == 0:
            return table(c, {d1: pos[d1], **fixed})
        return held1.at[(c, r1 - 1) + tuple(fixed.get(k, slice(None)) for k in range(3) if k != d1)]

    def phase1():
        for c in range(COLORS):
            d = ORDERS[c][0]
            send(table(c, {d: far[d]}), tie1.at[c], send_sem.at[0, c], recv1.at[c, 0], (stage, near_a[d]))
        for c in range(COLORS):
            d = ORDERS[c][0]
            send(table(c, {d: to_b[d]}), held1.at[c, 2], send_sem.at[0, c], recv1.at[c, 3], (stage, near_b[d]))
        for c in range(COLORS):
            d = ORDERS[c][0]
            send(table(c, {d: to_a[d]}), held1.at[c, 0], send_sem.at[0, c], recv1.at[c, 1], (stage, near_a[d]))

    def forward1():
        for c in range(COLORS):
            d = ORDERS[c][0]
            wait(tie1.at[c], recv1.at[c, 0])
            send(tie1.at[c], held1.at[c, 1], send_sem.at[3, c], recv1.at[c, 2], (stage, near_b[d]))

    def phase2(r1):
        for c in range(COLORS):
            d = ORDERS[c][1]
            if r1:
                wait(held1.at[c, r1 - 1], recv1.at[c, r1])
            send(from_first(c, r1, {d: to_b[d]}), held2.at[c, r1, 2], send_sem.at[1, c], recv2.at[c, r1, 3], (stage, near_b[d]))
            send(from_first(c, r1, {d: far[d]}), tie2.at[c, r1], send_sem.at[1, c], recv2.at[c, r1, 0], (stage, near_a[d]))
            send(from_first(c, r1, {d: to_a[d]}), held2.at[c, r1, 0], send_sem.at[1, c], recv2.at[c, r1, 1], (stage, near_a[d]))

    def forward2(r1):
        for c in range(COLORS):
            d = ORDERS[c][1]
            wait(tie2.at[c, r1], recv2.at[c, r1, 0])
            send(tie2.at[c, r1], held2.at[c, r1, 1], send_sem.at[4, c], recv2.at[c, r1, 2], (stage, near_b[d]))

    first_cols, last_cols = pl.ds(0, WIDE), pl.ds(WIDE, NARROW)

    def wide_from(c, r1, value):
        d2, d = ORDERS[c][1:]
        return (0, from_first(c, r1, {d2: pos[d2], d: value}).at[:, first_cols]), (pl.ds(1, 3), held2.at[c, r1, :, value, :, first_cols])

    def wide_ties(r1):
        for c in range(COLORS):
            d = ORDERS[c][2]
            for r2 in (1, 2, 3):
                wait(held2.at[c, r1, r2 - 1], recv2.at[c, r1, r2])
            for some, piece in wide_from(c, r1, far[d]):
                send(piece, tie3.at[c, r1, some].at[..., first_cols], send_sem.at[2, c], recv3_wide.at[c, r1], (stage, near_a[d]))

    def wide_to_b(r1):
        for c in range(COLORS):
            d = ORDERS[c][2]
            for some, piece in wide_from(c, r1, to_b[d]):
                send(piece, wide.at[r1, c, some, 3], send_sem.at[2, c], recv_wide.at[r1], (other, near_b[d]))

    def wide_to_a(r1):
        for c in range(COLORS):
            d = ORDERS[c][2]
            for some, piece in wide_from(c, r1, to_a[d]):
                send(piece, wide.at[r1, c, some, 1], send_sem.at[2, c], recv_wide.at[r1], (other, near_a[d]))
            for some, piece in wide_from(c, r1, pos[d]):
                send(piece, wide.at[r1, c, some, 0], send_sem.at[6, c], recv_wide.at[r1], (other, me))

    def wide_forward(r1):
        for c in range(COLORS):
            d = ORDERS[c][2]
            held = tie3.at[c, r1, :, :, first_cols]
            wait(held, recv3_wide.at[c, r1])
            send(held, wide.at[r1, c, :, 2], send_sem.at[5, c], recv_wide.at[r1], (other, near_b[d]))

    def narrow_from(c, value):
        d1, d2, d = ORDERS[c]
        kept = {d2: pos[d2], d: value}
        rest = tuple(kept[k] for k in range(3) if k != d1)
        return (
            (0, 0, table(c, {d1: pos[d1], **kept}).at[:, last_cols]),
            (pl.ds(1, 3), 0, held1.at[(c, slice(None)) + rest + (slice(None), last_cols)]),
            (slice(None), pl.ds(1, 3), held2.at[c, :, :, value, :, last_cols]),
        )

    def narrow_ties():
        for c in range(COLORS):
            d = ORDERS[c][2]
            for r1, r2, piece in narrow_from(c, far[d]):
                send(piece, tie3.at[c, r1, r2, :, last_cols], send_sem.at[2, c], recv3_narrow.at[c], (stage, near_a[d]))

    def narrow_to(values, near, role, own=False):
        for c in range(COLORS):
            d = ORDERS[c][2]
            for r1, r2, piece in narrow_from(c, values[d]):
                send(piece, narrow.at[(role + 1) % 4, r1, c, r2], send_sem.at[6 if own else 2, c], recv_narrow.at[(role + 1) % 4], (other, me if own else near[d]))

    def narrow_forward():
        for c in range(COLORS):
            d = ORDERS[c][2]
            held = tie3.at[c, :, :, :, last_cols]
            wait(held, recv3_narrow.at[c])
            send(held, narrow.at[3, :, c], send_sem.at[5, c], recv_narrow.at[3], (other, near_b[d]))

    side = [
        pltpu.make_async_remote_copy(src_ref=src, dst_ref=dst, send_sem=side_sem.at[0, k], recv_sem=side_sem.at[1, k], device_id=(other, me), device_id_type=MESH)
        for k, (src, dst) in enumerate(((ids_ref, ids_in), (slots_ref, slots_in), (gates_ref, gates_in), (h_ref, x_in)))
    ]
    local = [pltpu.make_async_copy(src, dst, local_sem.at[k]) for k, (src, dst) in enumerate(((norm_ref, norm_in), (wo_ref, wo_in)))]

    weights = (wq_ref, wk_ref, wv_ref)

    def load(k, i):
        slot = lax.rem(i, depth)
        return pltpu.make_async_copy(weights[k].at[pl.ds(pl.multiple_of(i * piece_rows, piece_rows), piece_rows)], raw.at[slot], raw_sem.at[slot])

    def flatten(k, start, stop):
        step = 64

        def body(i, carry):
            load(k, i).wait()
            for j in range(0, piece_rows, step):
                flat[k, pl.ds(pl.multiple_of(i * piece_rows + j, step), step), :] = raw[lax.rem(i, depth), pl.ds(j, step)].reshape(step, d_model)

            @pl.when(i + depth < pieces)
            def _():
                load(k, i + depth).start()

            return carry

        if start == 0:
            for i in range(depth):
                load(k, i).start()
        lax.fori_loop(start, stop, body, 0)

    def build_gates():
        for copy in side:
            copy.wait_recv()
        ids, slot = ids_in[...], slots_in[...]
        spot = slot - me * (COLORS * GROUP)
        colour = spot >> 3
        roles = []
        for k, shift in enumerate((4, 2, 0)):
            roles.append((sign[k] * (((ids >> shift) & 3) - pos[k])) & 3)
        first, second, third = [
            jnp.where(colour == 0, roles[ORDERS[0][k]], jnp.where(colour == 1, roles[ORDERS[1][k]], roles[ORDERS[2][k]]))
            for k in range(3)
        ]
        in_wide = (((first * COLORS + colour) * 4 + second) * 4 + third) * GROUP + (spot & 7)
        in_narrow = ((((third + 1) & 3) * 4 + first) * COLORS + colour) * (4 * GROUP) + second * GROUP + (spot & 7)
        columns = [jnp.where(slot >= 0, c, -1).astype(jnp.float32) for c in (in_wide, in_narrow)]
        both = jnp.concatenate([*columns, gates_in[...], jnp.zeros((104, seq), jnp.float32)], axis=0).T
        step = 256
        for which, g_mat in enumerate((g_wide, g_narrow)):
            for b in range(g_mat.shape[1] // step):
                col = (lax.broadcasted_iota(jnp.int32, (seq, step), 1) + b * step).astype(jnp.float32)
                val = jnp.zeros((seq, step), jnp.float32)
                for i in range(8):
                    at = which * 8 + i
                    val = jnp.where(both[:, at:at + 1] == col, both[:, 16 + i:17 + i], val)
                high = val.astype(jnp.bfloat16)
                rest = val - high.astype(jnp.float32)
                mid = rest.astype(jnp.bfloat16)
                low = (rest - mid.astype(jnp.float32)).astype(jnp.bfloat16)
                for third_of, piece in enumerate((high, mid, low)):
                    g_mat[third_of * seq:(third_of + 1) * seq, b * step:(b + 1) * step] = piece
        acc[...] = x_in[...].astype(jnp.float32)

    def add_rows(gates, blocks, cols):
        sums = jnp.dot(gates, blocks, preferred_element_type=jnp.float32)
        acc[:, cols] += sums[:seq] + (sums[seq:2 * seq] + sums[2 * seq:])

    def combine_wide(r1):
        wait(wide.at[r1], recv_wide.at[r1])
        count = COLORS * 16 * GROUP
        for b in range(WIDE // width):
            cols = slice(b * width, (b + 1) * width)
            add_rows(g_wide[:, r1 * count:(r1 + 1) * count], wide[r1, :, :, :, :, cols].reshape(count, width), cols)

    def combine_narrow(roles):
        for r in range(2 * roles, 2 * roles + 2):
            wait(narrow.at[r], recv_narrow.at[r])
        count = 2 * COLORS * 16 * GROUP
        blocks = narrow[2 * roles:2 * roles + 2].reshape(count, NARROW)
        add_rows(g_narrow[:, roles * count:(roles + 1) * count], blocks, slice(WIDE, d_model))

    def square_sum(lo, hi):
        total = jnp.zeros((seq, 1), jnp.float32)
        for b in range(lo, hi, width):
            y = acc[:, b:b + width].astype(jnp.bfloat16).astype(jnp.float32)
            acc[:, b:b + width] = y
            total += jnp.sum(y * y, axis=1, keepdims=True)
        return total

    def inverse_rms(total, count):
        return lax.rsqrt(total * (1.0 / count) + NORM_EPS)

    def scale(lo, hi, inv):
        for b in range(lo, hi, width):
            x_in[:, b:b + width] = (acc[:, b:b + width] * inv * norm_in[:, b:b + width]).astype(jnp.bfloat16)

    head = 128
    pair = 2 * head
    causal = lax.broadcasted_iota(jnp.int32, (seq, seq), 0) >= lax.broadcasted_iota(jnp.int32, (seq, seq), 1)

    def project_wide():
        for k in range(3):
            for b in range(0, d_model, pair):
                part[k, :, b:b + pair] = jnp.dot(x_in[:, :WIDE], flat[k, :WIDE, b:b + pair], preferred_element_type=jnp.float32)

    def project(k, p, ratio):
        cols = slice(p * pair, (p + 1) * pair)
        rest = jnp.dot(x_in[:, WIDE:], flat[k, WIDE:, cols], preferred_element_type=jnp.float32)
        qkv[k, :, cols] = (part[k, :, cols] * ratio + rest).astype(jnp.bfloat16)

    def softmax(cols):
        scores = jnp.where(causal, part[0, :, cols] * (head ** -0.5), -jnp.inf)
        grown = jnp.exp(scores - jnp.max(scores, axis=1, keepdims=True))
        qkv[0, :, cols] = (grown * (1.0 / jnp.sum(grown, axis=1, keepdims=True))).astype(jnp.bfloat16)

    def attend(ratio):
        spans = [slice(h * head, (h + 1) * head) for h in range(d_model // head)]
        for k in range(2):
            for p in range(d_model // pair):
                project(k, p, ratio)
        for cols in spans:
            part[0, :, cols] = lax.dot_general(qkv[0, :, cols], qkv[1, :, cols], (((1,), (1,)), ((), ())), preferred_element_type=jnp.float32)
        for p in range(d_model // pair):
            softmax(spans[2 * p])
            softmax(spans[2 * p + 1])
            project(2, p, ratio)
        for cols in spans:
            x_in[:, cols] = jnp.dot(qkv[0, :, cols], qkv[2, :, cols], preferred_element_type=jnp.float32).astype(jnp.bfloat16)

    phase1()
    for copy in side:
        copy.start()
    phase2(0)
    for copy in local:
        copy.start()
    build_gates()
    flatten(0, 0, pieces)
    flatten(1, 0, pieces // 2)
    forward1()
    phase2(3)
    flatten(1, pieces // 2, pieces)
    forward2(0)
    phase2(1)
    flatten(2, 0, pieces // 2)
    forward2(3)
    phase2(2)
    wide_ties(0)
    wide_to_b(0)
    wide_to_a(0)
    flatten(2, pieces // 2, pieces)
    forward2(1)
    wide_ties(3)
    wide_to_b(3)
    forward2(2)
    wide_forward(0)
    wide_to_a(3)
    wide_ties(1)
    wide_to_b(1)
    wide_forward(3)
    wide_ties(2)
    wide_to_b(2)
    wide_to_a(1)
    combine_wide(0)
    wide_forward(1)
    narrow_ties()
    narrow_to(to_b, near_b, 3)
    wide_to_a(2)
    combine_wide(3)
    narrow_to(to_a, near_a, 1)
    narrow_to(pos, None, 0, own=True)
    wide_forward(2)
    for copy in local:
        copy.wait()
    narrow_forward()
    combine_wide(1)
    combine_wide(2)
    wide_total = square_sum(0, WIDE)
    wide_inv = inverse_rms(wide_total, WIDE)
    scale(0, WIDE, wide_inv)
    project_wide()
    combine_narrow(0)
    combine_narrow(1)
    inv = inverse_rms(wide_total + square_sum(WIDE, d_model), d_model)
    scale(WIDE, d_model, inv)
    attend(jnp.where(wide_inv > 0.0, inv / wide_inv, 0.0))
    for b in range(d_model // pair):
        cols = slice(b * pair, (b + 1) * pair)
        out = jnp.dot(x_in[...], wo_in[:, cols], preferred_element_type=jnp.float32).astype(jnp.bfloat16)
        z_ref[:, cols] = (acc[:, cols] + out.astype(jnp.float32)).astype(jnp.bfloat16)

    for copy in side:
        copy.wait_send()
    for c in range(COLORS):
        for k, ref in enumerate((held1, held2, held2, tie1, tie2, tie3, tie3)):
            wait(ref.at[c], send_sem.at[k, c])


def run_stage(o_tab, ids, slots, gates, h, norm_w, wq, wk, wv, wo):
    seq, d = h.shape
    dma = pltpu.SemaphoreType.DMA
    block = (GROUP, d)
    piece = 128

    def buf(*lead):
        return pltpu.VMEM(lead + block, jnp.bfloat16)

    return pl.pallas_call(
        stage_kernel,
        out_shape=pltpu.VMEM((seq, d), jnp.bfloat16),
        in_specs=[pl.BlockSpec(memory_space=pl.ANY)] * 10,
        out_specs=pl.BlockSpec(memory_space=pltpu.VMEM),
        scratch_shapes=[
            pltpu.VMEM((4, COLORS, 4, 4, GROUP, WIDE), jnp.bfloat16),
            pltpu.VMEM((4, 4, COLORS, 4, GROUP, NARROW), jnp.bfloat16),
            buf(COLORS, 3, 4, 4),
            buf(COLORS, 4, 3, 4),
            buf(COLORS, 4, 4),
            buf(COLORS, 4, 4),
            buf(COLORS, 4, 4),
            pltpu.VMEM(ids.shape, jnp.int32),
            pltpu.VMEM(slots.shape, jnp.int32),
            pltpu.VMEM(gates.shape, jnp.float32),
            pltpu.VMEM((3 * seq, 64 * COLORS * GROUP), jnp.bfloat16),
            pltpu.VMEM((3 * seq, 64 * COLORS * GROUP), jnp.bfloat16),
            pltpu.VMEM((seq, d), jnp.float32),
            pltpu.VMEM(norm_w.shape, jnp.float32),
            pltpu.VMEM((3, d, d), jnp.bfloat16),
            pltpu.VMEM((d, d), jnp.bfloat16),
            pltpu.VMEM((3, piece) + wq.shape[1:], jnp.bfloat16),
            pltpu.VMEM((seq, d), jnp.bfloat16),
            pltpu.VMEM((3, seq, d), jnp.float32),
            pltpu.VMEM((3, seq, d), jnp.bfloat16),
            dma((2, 4)),
            dma((2,)),
            dma((3,)),
            dma((7, COLORS)),
            dma((COLORS, 4)),
            dma((COLORS, 4, 4)),
            dma((COLORS, 4)),
            dma((COLORS,)),
            dma((4,)),
            dma((4,)),
        ],
        compiler_params=pltpu.CompilerParams(collective_id=0, has_side_effects=True, vmem_limit_bytes=63 * 1024 * 1024),
        name='stage',
    )(o_tab, ids, slots, gates, h, norm_w, wq, wk, wv, wo)


def solution(mesh):
    tok_spec = P('pp', 'ep', None, None)
    wt_spec = P('pp', None, None, None)

    def device_step(expert_out, expert_ids, slot_ids, gate_vals, residual, norm_w, w_query, w_key, w_value, w_out):
        seq_len, d_model = residual.shape[2:]

        def choices(array):
            return array.reshape(seq_len, array.shape[3]).T

        result = run_stage(
            expert_out.reshape(SIDE, SIDE, SIDE, COLORS, GROUP, d_model),
            choices(expert_ids), choices(slot_ids), choices(gate_vals),
            residual.reshape(seq_len, d_model), norm_w, w_query[0], w_key[0], w_value[0], w_out[0].reshape(-1, d_model),
        )
        return result.reshape(residual.shape)

    return jax.shard_map(device_step, mesh=mesh, in_specs=(tok_spec, tok_spec, tok_spec, tok_spec, tok_spec, P('pp', None), wt_spec, wt_spec, wt_spec, wt_spec), out_specs=tok_spec, check_vma=False)
```

time: 84.6 us -> 84.2 us (level)
  no operation moved by 1% of the time
where the time goes in v6:
time: 84.2 us; the launch traced here: 83.7 us
  Pallas kernels  82.9 us (98%)
    pallas_call x1, Pallas kernels, run_stage(): pl.pallas_call(stage_kernel, out_shape=pltpu.VMEM((seq, d), jnp.bfloat16)...  82.9 us

profile of v6, /device:TPU:1, one launch (start us, length us, event | category | flops | bytes accessed | tf_op | source)
XLA Modules:
  0.0 83.7 jit_solution(3011308806697044691)
XLA Ops:
  0.0 82.9 %stage.1 = bf16[128,2048]{1,0:T(8,128)(2,1)S(1)} custom-call(bf16[4,4,4,3,8,2048]{5,4,3,2,1,0:T(8,128)(2,1)} %bitcast.21, s32[8,128]{1,0:T(8,128)} %bitcast.23, s32[8,128]{1,0:T(8,128)} %bitcast.24, f32[8,128]{1,0:T(8,128)} %bitcast.25, bf16[128,2048]{1,0:T(8,128)(2,1)} %bitcast.22, f32[1,2048]{1,0:T(1,128)} %norm_ref.1, bf16[2048,16,128]{2,1,0:T(8,128)(2,1)} %bitcast.17, ...), custom_call_target="tpu_custom_call" | custom-call | tf_op jit(solution)/shard_map/stage/pallas_call | solution.py:365
  82.9 0.8 copy.12

commit v7 on v6

--- a/solution.py
+++ b/solution.py
@@ -11,7 +11,7 @@
 GROUP = 8
 COLORS = 3
 ORDERS = ((2, 1, 0), (1, 0, 2), (0, 2, 1))
-WIDE, NARROW = 1536, 512
+WIDE, NARROW = 1280, 768
 
 
 def stage_kernel(o_ref, ids_ref, slots_ref, gates_ref, h_ref, norm_ref, wq_ref, wk_ref, wv_ref, wo_ref, z_ref, wide, narrow, held1, held2, tie1, tie2, tie3, ids_in, slots_in, gates_in, g_wide, g_narrow, acc, norm_in, flat, wo_in, raw, x_in, part, qkv, side_sem, local_sem, raw_sem, send_sem, recv1, recv2, recv3_wide, recv3_narrow, recv_wide, recv_narrow):
@@ -24,7 +24,6 @@
     to_b = [lax.rem(p - s + SIDE, SIDE) for p, s in zip(pos, sign)]
     far = [lax.rem(p + 2, SIDE) for p in pos]
     seq, d_model = x_in.shape
-    width = 512
     depth, piece_rows = raw.shape[:2]
     pieces = flat.shape[1] // piece_rows
 
@@ -226,22 +225,22 @@
     def combine_wide(r1):
         wait(wide.at[r1], recv_wide.at[r1])
         count = COLORS * 16 * GROUP
-        for b in range(WIDE // width):
-            cols = slice(b * width, (b + 1) * width)
-            add_rows(g_wide[:, r1 * count:(r1 + 1) * count], wide[r1, :, :, :, :, cols].reshape(count, width), cols)
+        for cols in spans(0, WIDE):
+            add_rows(g_wide[:, r1 * count:(r1 + 1) * count], wide[r1, :, :, :, :, cols].reshape(count, -1), cols)
 
     def combine_narrow(roles):
         for r in range(2 * roles, 2 * roles + 2):
             wait(narrow.at[r], recv_narrow.at[r])
         count = 2 * COLORS * 16 * GROUP
-        blocks = narrow[2 * roles:2 * roles + 2].reshape(count, NARROW)
-        add_rows(g_narrow[:, roles * count:(roles + 1) * count], blocks, slice(WIDE, d_model))
+        for cols in spans(0, NARROW):
+            blocks = narrow[2 * roles:2 * roles + 2, :, :, :, :, cols].reshape(count, -1)
+            add_rows(g_narrow[:, roles * count:(roles + 1) * count], blocks, slice(WIDE + cols.start, WIDE + cols.stop))
 
     def square_sum(lo, hi):
         total = jnp.zeros((seq, 1), jnp.float32)
-        for b in range(lo, hi, width):
-            y = acc[:, b:b + width].astype(jnp.bfloat16).astype(jnp.float32)
-            acc[:, b:b + width] = y
+        for cols in spans(lo, hi):
+            y = acc[:, cols].astype(jnp.bfloat16).astype(jnp.float32)
+            acc[:, cols] = y
             total += jnp.sum(y * y, axis=1, keepdims=True)
         return total
 
@@ -249,8 +248,8 @@
         return lax.rsqrt(total * (1.0 / count) + NORM_EPS)
 
     def scale(lo, hi, inv):
-        for b in range(lo, hi, width):
-            x_in[:, b:b + width] = (acc[:, b:b + width] * inv * norm_in[:, b:b + width]).astype(jnp.bfloat16)
+        for cols in spans(lo, hi):
+            x_in[:, cols] = (acc[:, cols] * inv * norm_in[:, cols]).astype(jnp.bfloat16)
 
     head = 128
     pair = 2 * head
@@ -272,17 +271,17 @@
         qkv[0, :, cols] = (grown * (1.0 / jnp.sum(grown, axis=1, keepdims=True))).astype(jnp.bfloat16)
 
     def attend(ratio):
-        spans = [slice(h * head, (h + 1) * head) for h in range(d_model // head)]
+        heads = [slice(h * head, (h + 1) * head) for h in range(d_model // head)]
         for k in range(2):
             for p in range(d_model // pair):
                 project(k, p, ratio)
-        for cols in spans:
+        for cols in heads:
             part[0, :, cols] = lax.dot_general(qkv[0, :, cols], qkv[1, :, cols], (((1,), (1,)), ((), ())), preferred_element_type=jnp.float32)
         for p in range(d_model // pair):
-            softmax(spans[2 * p])
-            softmax(spans[2 * p + 1])
+            softmax(heads[2 * p])
+            softmax(heads[2 * p + 1])
             project(2, p, ratio)
-        for cols in spans:
+        for cols in heads:
             x_in[:, cols] = jnp.dot(qkv[0, :, cols], qkv[2, :, cols], preferred_element_type=jnp.float32).astype(jnp.bfloat16)
 
     phase1()
@@ -353,6 +352,10 @@
             wait(ref.at[c], send_sem.at[k, c])
 
 
+def spans(lo, hi):
+    return [slice(b, min(b + 512, hi)) for b in range(lo, hi, 512)]
+
+
 def run_stage(o_tab, ids, slots, gates, h, norm_w, wq, wk, wv, wo):
     seq, d = h.shape
     dma = pltpu.SemaphoreType.DMA

time: 84.2 us -> 83.7 us (level)
  no operation moved by 1% of the time
where the time goes in v7:
time: 83.7 us; the launch traced here: 83.3 us
  Pallas kernels  82.5 us (99%)
    pallas_call x1, Pallas kernels, run_stage(): pl.pallas_call(stage_kernel, out_shape=pltpu.VMEM((seq, d), jnp.bfloat16)...  82.5 us

profile of v7, /device:TPU:1, one launch (start us, length us, event | category | flops | bytes accessed | tf_op | source)
XLA Modules:
  0.0 83.3 jit_solution(13264240186949539437)
XLA Ops:
  0.0 82.5 %stage.1 = bf16[128,2048]{1,0:T(8,128)(2,1)S(1)} custom-call(bf16[4,4,4,3,8,2048]{5,4,3,2,1,0:T(8,128)(2,1)} %bitcast.21, s32[8,128]{1,0:T(8,128)} %bitcast.23, s32[8,128]{1,0:T(8,128)} %bitcast.24, f32[8,128]{1,0:T(8,128)} %bitcast.25, bf16[128,2048]{1,0:T(8,128)(2,1)} %bitcast.22, f32[1,2048]{1,0:T(1,128)} %norm_ref.1, bf16[2048,16,128]{2,1,0:T(8,128)(2,1)} %bitcast.17, ...), custom_call_target="tpu_custom_call" | custom-call | tf_op jit(solution)/shard_map/stage/pallas_call | solution.py:368
  82.5 0.8 copy.12

commit v8 on v7

--- a/solution.py
+++ b/solution.py
@@ -11,7 +11,7 @@
 GROUP = 8
 COLORS = 3
 ORDERS = ((2, 1, 0), (1, 0, 2), (0, 2, 1))
-WIDE, NARROW = 1280, 768
+WIDE, NARROW = 1024, 512
 
 
 def stage_kernel(o_ref, ids_ref, slots_ref, gates_ref, h_ref, norm_ref, wq_ref, wk_ref, wv_ref, wo_ref, z_ref, wide, narrow, held1, held2, tie1, tie2, tie3, ids_in, slots_in, gates_in, g_wide, g_narrow, acc, norm_in, flat, wo_in, raw, x_in, part, qkv, side_sem, local_sem, raw_sem, send_sem, recv1, recv2, recv3_wide, recv3_narrow, recv_wide, recv_narrow):
@@ -61,7 +61,8 @@
     def phase1():
         for c in range(COLORS):
             d = ORDERS[c][0]
-            send(table(c, {d: far[d]}), tie1.at[c], send_sem.at[0, c], recv1.at[c, 0], (stage, near_a[d]))
+            for half in range(2):
+                send(table(c, {d: far[d], (d == 0) * 1: pl.ds(2 * half, 2)}), tie1.at[c, pl.ds(2 * half, 2)], send_sem.at[0, c], recv1.at[c, 4 * half], (stage, near_a[d]))
         for c in range(COLORS):
             d = ORDERS[c][0]
             send(table(c, {d: to_b[d]}), held1.at[c, 2], send_sem.at[0, c], recv1.at[c, 3], (stage, near_b[d]))
@@ -69,11 +70,12 @@
             d = ORDERS[c][0]
             send(table(c, {d: to_a[d]}), held1.at[c, 0], send_sem.at[0, c], recv1.at[c, 1], (stage, near_a[d]))
 
-    def forward1():
+    def forward1(half):
+        some = pl.ds(2 * half, 2)
         for c in range(COLORS):
             d = ORDERS[c][0]
-            wait(tie1.at[c], recv1.at[c, 0])
-            send(tie1.at[c], held1.at[c, 1], send_sem.at[3, c], recv1.at[c, 2], (stage, near_b[d]))
+            wait(tie1.at[c, some], recv1.at[c, 4 * half])
+            send(tie1.at[c, some], held1.at[c, 1, some], send_sem.at[3, c], recv1.at[c, 2], (stage, near_b[d]))
 
     def phase2(r1):
         for c in range(COLORS):
@@ -90,7 +92,9 @@
             wait(tie2.at[c, r1], recv2.at[c, r1, 0])
             send(tie2.at[c, r1], held2.at[c, r1, 1], send_sem.at[4, c], recv2.at[c, r1, 2], (stage, near_b[d]))
 
-    first_cols, last_cols = pl.ds(0, WIDE), pl.ds(WIDE, NARROW)
+    first_cols = pl.ds(0, WIDE)
+    narrow_at = (WIDE, WIDE + NARROW)
+    narrow_cols = [pl.ds(at, NARROW) for at in narrow_at]
 
     def wide_from(c, r1, value):
         d2, d = ORDERS[c][1:]
@@ -125,34 +129,35 @@
             wait(held, recv3_wide.at[c, r1])
             send(held, wide.at[r1, c, :, 2], send_sem.at[5, c], recv_wide.at[r1], (other, near_b[d]))
 
-    def narrow_from(c, value):
+    def narrow_from(n, c, value):
         d1, d2, d = ORDERS[c]
         kept = {d2: pos[d2], d: value}
         rest = tuple(kept[k] for k in range(3) if k != d1)
+        cols = narrow_cols[n]
         return (
-            (0, 0, table(c, {d1: pos[d1], **kept}).at[:, last_cols]),
-            (pl.ds(1, 3), 0, held1.at[(c, slice(None)) + rest + (slice(None), last_cols)]),
-            (slice(None), pl.ds(1, 3), held2.at[c, :, :, value, :, last_cols]),
+            (0, 0, table(c, {d1: pos[d1], **kept}).at[:, cols]),
+            (pl.ds(1, 3), 0, held1.at[(c, slice(None)) + rest + (slice(None), cols)]),
+            (slice(None), pl.ds(1, 3), held2.at[c, :, :, value, :, cols]),
         )
 
-    def narrow_ties():
-        for c in range(COLORS):
-            d = ORDERS[c][2]
-            for r1, r2, piece in narrow_from(c, far[d]):
-                send(piece, tie3.at[c, r1, r2, :, last_cols], send_sem.at[2, c], recv3_narrow.at[c], (stage, near_a[d]))
-
-    def narrow_to(values, near, role, own=False):
-        for c in range(COLORS):
-            d = ORDERS[c][2]
-            for r1, r2, piece in narrow_from(c, values[d]):
-                send(piece, narrow.at[(role + 1) % 4, r1, c, r2], send_sem.at[6 if own else 2, c], recv_narrow.at[(role + 1) % 4], (other, me if own else near[d]))
-
-    def narrow_forward():
-        for c in range(COLORS):
-            d = ORDERS[c][2]
-            held = tie3.at[c, :, :, :, last_cols]
-            wait(held, recv3_narrow.at[c])
-            send(held, narrow.at[3, :, c], send_sem.at[5, c], recv_narrow.at[3], (other, near_b[d]))
+    def narrow_ties(n):
+        for c in range(COLORS):
+            d = ORDERS[c][2]
+            for r1, r2, piece in narrow_from(n, c, far[d]):
+                send(piece, tie3.at[c, r1, r2, :, narrow_cols[n]], send_sem.at[2, c], recv3_narrow.at[n, c], (stage, near_a[d]))
+
+    def narrow_to(n, values, near, role, own=False):
+        for c in range(COLORS):
+            d = ORDERS[c][2]
+            for r1, r2, piece in narrow_from(n, c, values[d]):
+                send(piece, narrow.at[n, (role + 1) % 4, r1, c, r2], send_sem.at[6 if own else 2, c], recv_narrow.at[n, (role + 1) % 4], (other, me if own else near[d]))
+
+    def narrow_forward(n):
+        for c in range(COLORS):
+            d = ORDERS[c][2]
+            held = tie3.at[c, :, :, :, narrow_cols[n]]
+            wait(held, recv3_narrow.at[n, c])
+            send(held, narrow.at[n, 3, :, c], send_sem.at[5, c], recv_narrow.at[n, 3], (other, near_b[d]))
 
     side = [
         pltpu.make_async_remote_copy(src_ref=src, dst_ref=dst, send_sem=side_sem.at[0, k], recv_sem=side_sem.at[1, k], device_id=(other, me), device_id_type=MESH)
@@ -228,13 +233,12 @@
         for cols in spans(0, WIDE):
             add_rows(g_wide[:, r1 * count:(r1 + 1) * count], wide[r1, :, :, :, :, cols].reshape(count, -1), cols)
 
-    def combine_narrow(roles):
+    def combine_narrow(n, roles):
         for r in range(2 * roles, 2 * roles + 2):
-            wait(narrow.at[r], recv_narrow.at[r])
+            wait(narrow.at[n, r], recv_narrow.at[n, r])
         count = 2 * COLORS * 16 * GROUP
-        for cols in spans(0, NARROW):
-            blocks = narrow[2 * roles:2 * roles + 2, :, :, :, :, cols].reshape(count, -1)
-            add_rows(g_narrow[:, roles * count:(roles + 1) * count], blocks, slice(WIDE + cols.start, WIDE + cols.stop))
+        blocks = narrow[n, 2 * roles:2 * roles + 2].reshape(count, NARROW)
+        add_rows(g_narrow[:, roles * count:(roles + 1) * count], blocks, slice(narrow_at[n], narrow_at[n] + NARROW))
 
     def square_sum(lo, hi):
         total = jnp.zeros((seq, 1), jnp.float32)
@@ -260,10 +264,21 @@
             for b in range(0, d_model, pair):
                 part[k, :, b:b + pair] = jnp.dot(x_in[:, :WIDE], flat[k, :WIDE, b:b + pair], preferred_element_type=jnp.float32)
 
-    def project(k, p, ratio):
+    def project(k, p, n, ratio):
         cols = slice(p * pair, (p + 1) * pair)
-        rest = jnp.dot(x_in[:, WIDE:], flat[k, WIDE:, cols], preferred_element_type=jnp.float32)
-        qkv[k, :, cols] = (part[k, :, cols] * ratio + rest).astype(jnp.bfloat16)
+        rows = slice(narrow_at[n], narrow_at[n] + NARROW)
+        total = part[k, :, cols] * ratio + jnp.dot(x_in[:, rows], flat[k, rows, cols], preferred_element_type=jnp.float32)
+        if n == 0:
+            part[k, :, cols] = total
+        else:
+            qkv[k, :, cols] = total.astype(jnp.bfloat16)
+
+    def grow(total, inv, n):
+        stop = narrow_at[n] + NARROW
+        total = total + square_sum(narrow_at[n], stop)
+        new_inv = inverse_rms(total, stop)
+        scale(narrow_at[n], stop, new_inv)
+        return total, new_inv, jnp.where(inv > 0.0, new_inv / inv, 0.0)
 
     def softmax(cols):
         scores = jnp.where(causal, part[0, :, cols] * (head ** -0.5), -jnp.inf)
@@ -274,13 +289,13 @@
         heads = [slice(h * head, (h + 1) * head) for h in range(d_model // head)]
         for k in range(2):
             for p in range(d_model // pair):
-                project(k, p, ratio)
+                project(k, p, 1, ratio)
         for cols in heads:
             part[0, :, cols] = lax.dot_general(qkv[0, :, cols], qkv[1, :, cols], (((1,), (1,)), ((), ())), preferred_element_type=jnp.float32)
         for p in range(d_model // pair):
             softmax(heads[2 * p])
             softmax(heads[2 * p + 1])
-            project(2, p, ratio)
+            project(2, p, 1, ratio)
         for cols in heads:
             x_in[:, cols] = jnp.dot(qkv[0, :, cols], qkv[2, :, cols], preferred_element_type=jnp.float32).astype(jnp.bfloat16)
 
@@ -291,11 +306,12 @@
     for copy in local:
         copy.start()
     build_gates()
-    flatten(0, 0, pieces)
-    flatten(1, 0, pieces // 2)
-    forward1()
+    flatten(0, 0, pieces // 2)
+    forward1(0)
+    flatten(0, pieces // 2, pieces)
+    forward1(1)
     phase2(3)
-    flatten(1, pieces // 2, pieces)
+    flatten(1, 0, pieces)
     forward2(0)
     phase2(1)
     flatten(2, 0, pieces // 2)
@@ -303,43 +319,52 @@
     phase2(2)
     wide_ties(0)
     wide_to_b(0)
-    wide_to_a(0)
     flatten(2, pieces // 2, pieces)
     forward2(1)
     wide_ties(3)
     wide_to_b(3)
+    wide_to_a(0)
     forward2(2)
-    wide_forward(0)
-    wide_to_a(3)
     wide_ties(1)
     wide_to_b(1)
+    wide_to_a(3)
+    wide_forward(0)
     wide_forward(3)
     wide_ties(2)
     wide_to_b(2)
     wide_to_a(1)
+    narrow_ties(0)
+    wide_to_a(2)
+    narrow_ties(1)
+    for n in range(2):
+        narrow_to(n, to_a, near_a, 1)
+        narrow_to(n, pos, None, 0, own=True)
+    wide_forward(1)
+    narrow_to(0, to_b, near_b, 3)
     combine_wide(0)
-    wide_forward(1)
-    narrow_ties()
-    narrow_to(to_b, near_b, 3)
-    wide_to_a(2)
-    combine_wide(3)
-    narrow_to(to_a, near_a, 1)
-    narrow_to(pos, None, 0, own=True)
     wide_forward(2)
+    narrow_to(1, to_b, near_b, 3)
     for copy in local:
         copy.wait()
-    narrow_forward()
+    combine_wide(3)
     combine_wide(1)
+    narrow_forward(0)
     combine_wide(2)
-    wide_total = square_sum(0, WIDE)
-    wide_inv = inverse_rms(wide_total, WIDE)
-    scale(0, WIDE, wide_inv)
+    narrow_forward(1)
+    total = square_sum(0, WIDE)
+    inv = inverse_rms(total, WIDE)
+    scale(0, WIDE, inv)
     project_wide()
-    combine_narrow(0)
-    combine_narrow(1)
-    inv = inverse_rms(wide_total + square_sum(WIDE, d_model), d_model)
-    scale(WIDE, d_model, inv)
-    attend(jnp.where(wide_inv > 0.0, inv / wide_inv, 0.0))
+    combine_narrow(0, 0)
+    combine_narrow(0, 1)
+    total, inv, ratio = grow(total, inv, 0)
+    for k in range(3):
+        for p in range(d_model // pair):
+            project(k, p, 0, ratio)
+    combine_narrow(1, 0)
+    combine_narrow(1, 1)
+    total, inv, ratio = grow(total, inv, 1)
+    attend(ratio)
     for b in range(d_model // pair):
         cols = slice(b * pair, (b + 1) * pair)
         out = jnp.dot(x_in[...], wo_in[:, cols], preferred_element_type=jnp.float32).astype(jnp.bfloat16)
@@ -372,7 +397,7 @@
         out_specs=pl.BlockSpec(memory_space=pltpu.VMEM),
         scratch_shapes=[
             pltpu.VMEM((4, COLORS, 4, 4, GROUP, WIDE), jnp.bfloat16),
-            pltpu.VMEM((4, 4, COLORS, 4, GROUP, NARROW), jnp.bfloat16),
+            pltpu.VMEM((2, 4, 4, COLORS, 4, GROUP, NARROW), jnp.bfloat16),
             buf(COLORS, 3, 4, 4),
             buf(COLORS, 4, 3, 4),
             buf(COLORS, 4, 4),
@@ -395,12 +420,12 @@
             dma((2,)),
             dma((3,)),
             dma((7, COLORS)),
-            dma((COLORS, 4)),
+            dma((COLORS, 5)),
             dma((COLORS, 4, 4)),
             dma((COLORS, 4)),
-            dma((COLORS,)),
+            dma((2, COLORS)),
             dma((4,)),
-            dma((4,)),
+            dma((2, 4)),
         ],
         compiler_params=pltpu.CompilerParams(collective_id=0, has_side_effects=True, vmem_limit_bytes=63 * 1024 * 1024),
         name='stage',

time: 83.7 us -> 82.3 us (0.983)
  Pallas kernels: 82.5 us -> 81 us
    pallas_call x1, Pallas kernels: 82.5 us -> 81 us  [run_stage(): pl.pallas_call(stage_kernel, out_shape=pltpu.VMEM((seq, d), jnp.bfloat16)...]
where the time goes in v8:
time: 82.3 us; the launch traced here: 81.8 us
  Pallas kernels  81 us (98%)
    pallas_call x1, Pallas kernels, run_stage(): pl.pallas_call(stage_kernel, out_shape=pltpu.VMEM((seq, d), jnp.bfloat16)...  81 us

profile of v8, /device:TPU:1, one launch (start us, length us, event | category | flops | bytes accessed | tf_op | source)
XLA Modules:
  0.0 81.8 jit_solution(11179783844217798110)
XLA Ops:
  0.0 81.0 %stage.1 = bf16[128,2048]{1,0:T(8,128)(2,1)S(1)} custom-call(bf16[4,4,4,3,8,2048]{5,4,3,2,1,0:T(8,128)(2,1)} %bitcast.21, s32[8,128]{1,0:T(8,128)} %bitcast.23, s32[8,128]{1,0:T(8,128)} %bitcast.24, f32[8,128]{1,0:T(8,128)} %bitcast.25, bf16[128,2048]{1,0:T(8,128)(2,1)} %bitcast.22, f32[1,2048]{1,0:T(1,128)} %norm_ref.1, bf16[2048,16,128]{2,1,0:T(8,128)(2,1)} %bitcast.17, ...), custom_call_target="tpu_custom_call" | custom-call | tf_op jit(solution)/shard_map/stage/pallas_call | solution.py:393
  81.0 0.8 copy.12

commit v9 on v0

v9 whole, which is shorter than its diff:
```python
import jax
import jax.numpy as jnp
from jax import lax
from jax.experimental import pallas as pl
from jax.experimental.pallas import tpu as pltpu
from jax.sharding import PartitionSpec as P

NORM_EPS = 1e-6
MESH = pl.DeviceIdType.MESH
SIDE = 4
COLORS = 3
SLOTS = 24
ORDERS = ((2, 1, 0), (1, 0, 2), (0, 2, 1))
WIDTHS = (640, 640, 768)
STARTS = (0, 640, 1280)
COLS = [slice(at, at + w) for at, w in zip(STARTS, WIDTHS)]
SPANS = [pl.ds(at, w) for at, w in zip(STARTS, WIDTHS)]
HELD = 16 * SLOTS
LOW, HIGH = pl.ds(0, 64), pl.ds(64, 64)


def stage_kernel(o_ref, ids_ref, slots_ref, gates_ref, h_ref, norm_ref, wq_ref, wk_ref, wv_ref, wo_ref, z_ref, *scratch):
    held1, tie1, held2, tie2, mine = [scratch[3 * k:3 * k + 3] for k in range(5)]
    (sums, tin, got, ids_in, slots_in, gates_in, g_mat, norm_in, flat, wo_in, raw, x_in, qkv,
     kg_sem, side_sem, local_sem, mine_sem, raw_sem, send_sem, recv1, recv2, tin_sem, got_sem) = scratch[15:]
    stage = lax.axis_index('pp')
    me = lax.axis_index('ep')
    other = 1 - stage
    pos = (me // 16, (me // 4) % 4, me % 4)
    sign = [1 - 2 * (p % 2) for p in pos]
    to_a = [lax.rem(p + s + SIDE, SIDE) for p, s in zip(pos, sign)]
    to_b = [lax.rem(p - s + SIDE, SIDE) for p, s in zip(pos, sign)]
    far = [lax.rem(p + 2, SIDE) for p in pos]
    seq, d_model = x_in.shape
    depth, piece_rows = raw.shape[:2]
    pieces = flat.shape[1] // piece_rows

    def rank(axis, value):
        z, y, x = [value if k == axis else p for k, p in enumerate(pos)]
        return z * 16 + y * 4 + x

    near_a = [rank(k, to_a[k]) for k in range(3)]
    near_b = [rank(k, to_b[k]) for k in range(3)]
    remote = [rank(k, far[k]) for k in range(3)]

    barrier = pltpu.get_barrier_semaphore()
    peers = [(other, me)]
    for k in range(3):
        peers.append((stage, remote[k]))
        for where in (near_a[k], near_b[k]):
            peers += [(stage, where), (other, where)]
    for peer in peers:
        pl.semaphore_signal(barrier, inc=1, device_id=peer, device_id_type=MESH)
    pl.semaphore_wait(barrier, len(peers))

    def copy_to(src, dst, send_s, recv_s, peer):
        return pltpu.make_async_remote_copy(src_ref=src, dst_ref=dst, send_sem=send_s, recv_sem=recv_s, device_id=peer, device_id_type=MESH)

    def send(*args):
        copy_to(*args).start()

    def wait(ref, sem):
        pltpu.make_async_copy(ref, ref, sem).wait()

    def table(c, fixed):
        return o_ref.at[tuple(fixed.get(k, slice(None)) for k in range(3)) + (slice(None), SPANS[c])]

    def from_first(c, r1, fixed):
        d1 = ORDERS[c][0]
        if r1 == 0:
            return table(c, {d1: pos[d1], **fixed})
        return held1[c].at[(r1 - 1,) + tuple(fixed.get(k, slice(None)) for k in range(3) if k != d1)]

    def phase1():
        for c in range(COLORS):
            d = ORDERS[c][0]
            for half in range(2):
                some = pl.ds(2 * half, 2)
                send(table(c, {d: far[d], (d == 0) * 1: some}), tie1[c].at[some], send_sem.at[0, c], recv1.at[c, 4 * half], (stage, near_a[d]))
        for c in range(COLORS):
            d = ORDERS[c][0]
            send(table(c, {d: to_b[d]}), held1[c].at[2], send_sem.at[0, c], recv1.at[c, 3], (stage, near_b[d]))
        for c in range(COLORS):
            d = ORDERS[c][0]
            send(table(c, {d: to_a[d]}), held1[c].at[0], send_sem.at[0, c], recv1.at[c, 1], (stage, near_a[d]))

    def forward1(half):
        some = pl.ds(2 * half, 2)
        for c in range(COLORS):
            d = ORDERS[c][0]
            wait(tie1[c].at[some], recv1.at[c, 4 * half])
            send(tie1[c].at[some], held1[c].at[1, some], send_sem.at[3, c], recv1.at[c, 2], (stage, near_b[d]))

    def phase2(r1):
        for c in range(COLORS):
            d = ORDERS[c][1]
            if r1:
                wait(held1[c].at[r1 - 1], recv1.at[c, r1])
            send(from_first(c, r1, {d: to_b[d]}), held2[c].at[r1, 2], send_sem.at[1, c], recv2.at[c, r1, 3], (stage, near_b[d]))
            send(from_first(c, r1, {d: far[d]}), tie2[c].at[r1], send_sem.at[1, c], recv2.at[c, r1, 0], (stage, near_a[d]))
            send(from_first(c, r1, {d: to_a[d]}), held2[c].at[r1, 0], send_sem.at[1, c], recv2.at[c, r1, 1], (stage, near_a[d]))

    def forward2(r1):
        for c in range(COLORS):
            d = ORDERS[c][1]
            wait(tie2[c].at[r1], recv2.at[c, r1, 0])
            send(tie2[c].at[r1], held2[c].at[r1, 1], send_sem.at[4, c], recv2.at[c, r1, 2], (stage, near_b[d]))

    def partial(c, role):
        d1, d2, d = ORDERS[c]
        value = (pos, to_a, far, to_b)[role][d]
        kept = {d2: pos[d2], d: value}
        near = held1[c][(slice(None),) + tuple(kept[k] for k in range(3) if k != d1)]
        blocks = jnp.concatenate([held2[c][:, :, value].reshape(12 * SLOTS, -1), near.reshape(3 * SLOTS, -1), mine[c][value]], axis=0)
        part = jnp.dot(g_mat[c * 4 + role], blocks, preferred_element_type=jnp.float32)
        sums[role, :, COLS[c]] = part[:seq] + (part[seq:2 * seq] + part[2 * seq:])

    def send_sums(c, role):
        d = ORDERS[c][2]
        if role == 2:
            send(sums.at[2, LOW, SPANS[c]], tin.at[LOW, SPANS[c]], send_sem.at[2, c], tin_sem.at[c, 0], (stage, near_a[d]))
            send(sums.at[2, HIGH, SPANS[c]], tin.at[HIGH, SPANS[c]], send_sem.at[2, c], tin_sem.at[c, 1], (stage, near_b[d]))
        elif role == 3:
            send(sums.at[3, HIGH, SPANS[c]], got.at[2, HIGH, SPANS[c]], send_sem.at[2, c], got_sem.at[2, c], (other, near_b[d]))
        elif role == 1:
            send(sums.at[1, LOW, SPANS[c]], got.at[1, LOW, SPANS[c]], send_sem.at[2, c], got_sem.at[1, c], (other, near_a[d]))
        else:
            send(sums.at[0, :, SPANS[c]], got.at[0, :, SPANS[c]], send_sem.at[5, c], got_sem.at[0, c], (other, me))

    def merge(c, low):
        wait(tin.at[LOW if low else HIGH, SPANS[c]], tin_sem.at[c, 0 if low else 1])
        role, rows = (3, slice(0, 64)) if low else (1, slice(64, 128))
        sums[role, rows, COLS[c]] += tin[rows, COLS[c]]

    def send_merged(c, low):
        d = ORDERS[c][2]
        if low:
            send(sums.at[3, LOW, SPANS[c]], got.at[2, LOW, SPANS[c]], send_sem.at[2, c], got_sem.at[2, c], (other, near_b[d]))
        else:
            send(sums.at[1, HIGH, SPANS[c]], got.at[1, HIGH, SPANS[c]], send_sem.at[2, c], got_sem.at[1, c], (other, near_a[d]))

    choices = ((ids_ref, ids_in), (slots_ref, slots_in), (gates_ref, gates_in))

    def send_choices():
        for k, (src, dst) in enumerate(choices):
            pltpu.make_async_copy(src, dst.at[9], local_sem.at[2 + k]).start()
            for axis in range(3):
                for role, peer in ((1, near_a[axis]), (2, remote[axis]), (3, near_b[axis])):
                    send(src, dst.at[axis * 3 + role - 1], kg_sem.at[0, k], kg_sem.at[1, k], (stage, peer))

    side = copy_to(h_ref, x_in, side_sem.at[0], side_sem.at[1], (other, me))
    local = [pltpu.make_async_copy(src, dst, local_sem.at[k]) for k, (src, dst) in enumerate(((norm_ref, norm_in), (wo_ref, wo_in)))]
    own = [pltpu.make_async_copy(table(c, {ORDERS[c][0]: pos[ORDERS[c][0]], ORDERS[c][1]: pos[ORDERS[c][1]]}), mine[c], mine_sem.at[c]) for c in range(COLORS)]

    def build_gates():
        for k, (src, dst) in enumerate(choices):
            pltpu.make_async_copy(src, dst.at[9], local_sem.at[2 + k]).wait()
            wait(dst.at[pl.ds(0, 9)], kg_sem.at[1, k])
        columns = []
        for c in range(COLORS):
            d1, d2, d = ORDERS[c]
            for role in range(4):
                value = (pos, to_a, far, to_b)[role][d]
                which = 9 if role == 0 else d * 3 + role - 1
                ids, slot = ids_in[which], slots_in[which]
                at = [(ids >> shift) & 3 for shift in (4, 2, 0)]
                first, second = [(sign[k] * (at[k] - pos[k])) & 3 for k in (d1, d2)]
                block = jnp.where(second > 0, first * 3 + second - 1, jnp.where(first > 0, 11 + first, 15))
                column = block * SLOTS + slot - rank(d, value) * SLOTS
                columns.append(jnp.where((slot >= 0) & (at[d] == pos[d]), column, -1).astype(jnp.float32))
        places = jnp.concatenate(columns + [jnp.zeros((32, seq), jnp.float32)], axis=0).T
        gates = jnp.concatenate([gates_in[k] for k in range(10)] + [jnp.zeros((48, seq), jnp.float32)], axis=0).T
        step = 128
        for c in range(COLORS):
            for role in range(4):
                g = 8 * (9 if role == 0 else ORDERS[c][2] * 3 + role - 1)
                p = 8 * (c * 4 + role)
                for b in range(0, HELD, step):
                    col = (lax.broadcasted_iota(jnp.int32, (seq, step), 1) + b).astype(jnp.float32)
                    val = jnp.zeros((seq, step), jnp.float32)
                    for i in range(8):
                        val = jnp.where(places[:, p + i:p + i + 1] == col, gates[:, g + i:g + i + 1], val)
                    high = val.astype(jnp.bfloat16)
                    rest = val - high.astype(jnp.float32)
                    mid = rest.astype(jnp.bfloat16)
                    low = (rest - mid.astype(jnp.float32)).astype(jnp.bfloat16)
                    for k, piece in enumerate((high, mid, low)):
                        g_mat[c * 4 + role, k * seq:(k + 1) * seq, b:b + step] = piece

    weights = (wq_ref, wk_ref, wv_ref)

    def load(k, i):
        slot = lax.rem(i, depth)
        return pltpu.make_async_copy(weights[k].at[pl.ds(pl.multiple_of(i * piece_rows, piece_rows), piece_rows)], raw.at[slot], raw_sem.at[slot])

    def flatten(k, start, stop):
        step = 64

        def body(i, carry):
            load(k, i).wait()
            for j in range(0, piece_rows, step):
                flat[k, pl.ds(pl.multiple_of(i * piece_rows + j, step), step), :] = raw[lax.rem(i, depth), pl.ds(j, step)].reshape(step, d_model)

            @pl.when(i + depth < pieces)
            def _():
                load(k, i + depth).start()

            return carry

        if start == 0:
            for i in range(depth):
                load(k, i).start()
        lax.fori_loop(start, stop, body, 0)

    head = 128
    pair = 2 * head
    causal = lax.broadcasted_iota(jnp.int32, (seq, seq), 0) >= lax.broadcasted_iota(jnp.int32, (seq, seq), 1)

    def norm():
        side.wait_recv()
        total = jnp.zeros((seq, 1), jnp.float32)
        for c in range(COLORS):
            for slot in range(3):
                wait(got.at[slot, :, SPANS[c]], got_sem.at[slot, c])
        for cols in spans(0, d_model):
            y = x_in[:, cols].astype(jnp.float32) + (got[0, :, cols] + (got[1, :, cols] + got[2, :, cols]))
            y = y.astype(jnp.bfloat16).astype(jnp.float32)
            got[0, :, cols] = y
            total += jnp.sum(y * y, axis=1, keepdims=True)
        inv = lax.rsqrt(total * (1.0 / d_model) + NORM_EPS)
        for cols in spans(0, d_model):
            x_in[:, cols] = (got[0, :, cols] * inv * norm_in[:, cols]).astype(jnp.bfloat16)

    def project(k, p):
        cols = slice(p * pair, (p + 1) * pair)
        qkv[k, :, cols] = jnp.dot(x_in[...], flat[k, :, cols], preferred_element_type=jnp.float32).astype(jnp.bfloat16)

    def softmax(cols):
        scores = jnp.where(causal, tin[:, cols] * (head ** -0.5), -jnp.inf)
        grown = jnp.exp(scores - jnp.max(scores, axis=1, keepdims=True))
        qkv[0, :, cols] = (grown * (1.0 / jnp.sum(grown, axis=1, keepdims=True))).astype(jnp.bfloat16)

    def attend():
        heads = [slice(h * head, (h + 1) * head) for h in range(d_model // head)]
        for k in range(2):
            for p in range(d_model // pair):
                project(k, p)
        for cols in heads:
            tin[:, cols] = lax.dot_general(qkv[0, :, cols], qkv[1, :, cols], (((1,), (1,)), ((), ())), preferred_element_type=jnp.float32)
        for p in range(d_model // pair):
            softmax(heads[2 * p])
            softmax(heads[2 * p + 1])
            project(2, p)
        for cols in heads:
            x_in[:, cols] = jnp.dot(qkv[0, :, cols], qkv[2, :, cols], preferred_element_type=jnp.float32).astype(jnp.bfloat16)

    phase1()
    send_choices()
    side.start()
    phase2(0)
    for copy in local + own:
        copy.start()
    build_gates()
    flatten(0, 0, pieces // 4)
    forward1(0)
    flatten(0, pieces // 4, pieces)
    forward1(1)
    phase2(3)
    flatten(1, 0, pieces)
    forward2(0)
    phase2(1)
    flatten(2, 0, pieces // 2)
    forward2(3)
    phase2(2)
    flatten(2, pieces // 2, pieces)
    forward2(1)
    for copy in own:
        copy.wait()
    forward2(2)
    for c in range(COLORS):
        for r1 in range(4):
            for r2 in (1, 2, 3):
                wait(held2[c].at[r1, r2 - 1], recv2.at[c, r1, r2])
    before = None
    for role in (2, 3, 1, 0):
        for c in range(COLORS):
            partial(c, role)
            if before is not None:
                send_sums(*before)
            before = (c, role)
    send_sums(*before)
    before = None
    for low in (True, False):
        for c in range(COLORS):
            merge(c, low)
            if before is not None:
                send_merged(*before)
            before = (c, low)
    for copy in local:
        copy.wait()
    send_merged(*before)
    norm()
    attend()
    for p in range(d_model // pair):
        cols = slice(p * pair, (p + 1) * pair)
        out = jnp.dot(x_in[...], wo_in[:, cols], preferred_element_type=jnp.float32).astype(jnp.bfloat16)
        z_ref[:, cols] = (got[0, :, cols] + out.astype(jnp.float32)).astype(jnp.bfloat16)

    side.wait_send()
    for k, (src, dst) in enumerate(choices):
        wait(dst.at[pl.ds(0, 9)], kg_sem.at[0, k])
    for c in range(COLORS):
        wait(held1[c], send_sem.at[0, c])
        wait(held2[c], send_sem.at[1, c])
        wait(sums.at[pl.ds(1, 3), :, SPANS[c]], send_sem.at[2, c])
        wait(tie1[c], send_sem.at[3, c])
        wait(tie2[c], send_sem.at[4, c])
        wait(sums.at[0, :, SPANS[c]], send_sem.at[5, c])


def spans(lo, hi):
    return [slice(b, min(b + 512, hi)) for b in range(lo, hi, 512)]


def run_stage(o_tab, ids, slots, gates, h, norm_w, wq, wk, wv, wo):
    seq, d = h.shape
    dma = pltpu.SemaphoreType.DMA
    piece = 128

    def per_colour(*lead):
        return [pltpu.VMEM(lead + (SLOTS, w), jnp.bfloat16) for w in WIDTHS]

    return pl.pallas_call(
        stage_kernel,
        out_shape=pltpu.VMEM((seq, d), jnp.bfloat16),
        in_specs=[pl.BlockSpec(memory_space=pl.ANY)] * 10,
        out_specs=pl.BlockSpec(memory_space=pltpu.VMEM),
        scratch_shapes=[
            *per_colour(3, 4, 4),
            *per_colour(4, 4),
            *per_colour(4, 3, 4),
            *per_colour(4, 4),
            *per_colour(4),
            pltpu.VMEM((4, seq, d), jnp.float32),
            pltpu.VMEM((seq, d), jnp.float32),
            pltpu.VMEM((3, seq, d), jnp.float32),
            pltpu.VMEM((10,) + ids.shape, jnp.int32),
            pltpu.VMEM((10,) + slots.shape, jnp.int32),
            pltpu.VMEM((10,) + gates.shape, jnp.float32),
            pltpu.VMEM((4 * COLORS, 3 * seq, HELD), jnp.bfloat16),
            pltpu.VMEM(norm_w.shape, jnp.float32),
            pltpu.VMEM((3, d, d), jnp.bfloat16),
            pltpu.VMEM((d, d), jnp.bfloat16),
            pltpu.VMEM((3, piece) + wq.shape[1:], jnp.bfloat16),
            pltpu.VMEM((seq, d), jnp.bfloat16),
            pltpu.VMEM((3, seq, d), jnp.bfloat16),
            dma((2, 3)),
            dma((2,)),
            dma((5,)),
            dma((COLORS,)),
            dma((3,)),
            dma((6, COLORS)),
            dma((COLORS, 5)),
            dma((COLORS, 4, 4)),
            dma((COLORS, 2)),
            dma((3, COLORS)),
        ],
        compiler_params=pltpu.CompilerParams(collective_id=0, has_side_effects=True, vmem_limit_bytes=66400000),
        name='stage',
    )(o_tab, ids, slots, gates, h, norm_w, wq, wk, wv, wo)


def solution(mesh):
    tok_spec = P('pp', 'ep', None, None)
    wt_spec = P('pp', None, None, None)

    def device_step(expert_out, expert_ids, slot_ids, gate_vals, residual, norm_w, w_query, w_key, w_value, w_out):
        seq_len, d_model = residual.shape[2:]

        def choices(array):
            return array.reshape(seq_len, array.shape[3]).T

        result = run_stage(
            expert_out.reshape(SIDE, SIDE, SIDE, SLOTS, d_model),
            choices(expert_ids), choices(slot_ids), choices(gate_vals),
            residual.reshape(seq_len, d_model), norm_w, w_query[0], w_key[0], w_value[0], w_out[0].reshape(-1, d_model),
        )
        return result.reshape(residual.shape)

    return jax.shard_map(device_step, mesh=mesh, in_specs=(tok_spec, tok_spec, tok_spec, tok_spec, tok_spec, P('pp', None), wt_spec, wt_spec, wt_spec, wt_spec), out_specs=tok_spec, check_vma=False)
```

time: 281 us -> 99 us (0.35); the launches traced: 278 us -> 98.5 us
  local copies, waits for them, and re-layouts: 103 us -> 0.8 us
  Pallas kernels: 0 us -> 97.7 us
  waiting for transfers between devices: 90 us -> 0 us
  other arithmetic: 46 us -> 0 us
  matrix products: 20.9 us -> 0 us
  starting transfers between devices: 17.8 us -> 0 us
    pallas_call x0 -> x1, Pallas kernels: none -> 97.7 us  [run_stage(): pl.pallas_call(stage_kernel, out_shape=pltpu.VMEM((seq, d), jnp.bfloat16)...]
    all_to_all x1 -> x0, waiting for transfers between devices: 88.5 us -> none  [device_step(): returned = lax.all_to_all(expert_out, 'ep', 2, 1, tiled=True)]
    unnamed x15 -> x1, local copies, waits for them, and re-layouts: 75.9 us -> 0.8 us
    unnamed x1 -> x0, other arithmetic: 38.9 us -> none
    gather x4 -> x0, local copies, waits for them, and re-layouts: 26.9 us -> none  [gated_sum(): exp_rows[id_blk, pos_blk]]
    dot_general x4 -> x0, matrix products: 20.9 us -> none  [the longest x1 5.84 us: attention_block(): jnp.einsum('crif,ife->cre', attn_out, w_out, preferred_element_type=jnp.f...]
    all_to_all x1 -> x0, starting transfers between devices: 12.5 us -> none  [device_step(): returned = lax.all_to_all(expert_out, 'ep', 2, 1, tiled=True)]
    reduce_sum x2 -> x0, other arithmetic: 6.71 us -> none  [the longest x1 6.53 us: gated_sum(): jnp.sum(weight[..., None] * picked.astype(jnp.float32), axis=3)]
  transfers between devices with their start and end apart: 2 -> 0, of which waited for: 2 -> 0; matrix products, arithmetic and copies ran while one was open for 0% -> 0% of each run, Pallas kernels for 0% -> 0%
where the time goes in v9:
time: 99 us; the launch traced here: 98.5 us
  Pallas kernels  97.7 us (99%)
    pallas_call x1, Pallas kernels, run_stage(): pl.pallas_call(stage_kernel, out_shape=pltpu.VMEM((seq, d), jnp.bfloat16)...  97.7 us

profile of v9, /device:TPU:1, one launch (start us, length us, event | category | flops | bytes accessed | tf_op | source)
XLA Modules:
  0.0 98.5 jit_solution(5265659485140413026)
XLA Ops:
  0.0 97.7 %stage.1 = bf16[128,2048]{1,0:T(8,128)(2,1)S(1)} custom-call(bf16[4,4,4,24,2048]{4,3,2,1,0:T(8,128)(2,1)} %bitcast.21, s32[8,128]{1,0:T(8,128)} %bitcast.23, s32[8,128]{1,0:T(8,128)} %bitcast.24, f32[8,128]{1,0:T(8,128)} %bitcast.25, bf16[128,2048]{1,0:T(8,128)(2,1)} %bitcast.22, f32[1,2048]{1,0:T(1,128)} %norm_ref.1, bf16[2048,16,128]{2,1,0:T(8,128)(2,1)} %bitcast.17, ...), custom_call_target="tpu_custom_call" | custom-call | tf_op jit(solution)/shard_map/stage/pallas_call | solution.py:333
  97.7 0.8 copy.12

commit v10 on v9

--- a/solution.py
+++ b/solution.py
@@ -254,8 +254,8 @@
         for cols in heads:
             x_in[:, cols] = jnp.dot(qkv[0, :, cols], qkv[2, :, cols], preferred_element_type=jnp.float32).astype(jnp.bfloat16)
 
+    send_choices()
     phase1()
-    send_choices()
     side.start()
     phase2(0)
     for copy in local + own:

time: 99 us -> 81.2 us (0.82)
  Pallas kernels: 97.7 us -> 79.9 us
    pallas_call x1, Pallas kernels: 97.7 us -> 79.9 us  [run_stage(): pl.pallas_call(stage_kernel, out_shape=pltpu.VMEM((seq, d), jnp.bfloat16)...]
where the time goes in v10:
time: 81.2 us; the launch traced here: 80.7 us
  Pallas kernels  79.9 us (98%)
    pallas_call x1, Pallas kernels, run_stage(): pl.pallas_call(stage_kernel, out_shape=pltpu.VMEM((seq, d), jnp.bfloat16)...  79.9 us

profile of v10, /device:TPU:1, one launch (start us, length us, event | category | flops | bytes accessed | tf_op | source)
XLA Modules:
  0.0 80.7 jit_solution(583544699107831969)
XLA Ops:
  0.0 79.9 %stage.1 = bf16[128,2048]{1,0:T(8,128)(2,1)S(1)} custom-call(bf16[4,4,4,24,2048]{4,3,2,1,0:T(8,128)(2,1)} %bitcast.21, s32[8,128]{1,0:T(8,128)} %bitcast.23, s32[8,128]{1,0:T(8,128)} %bitcast.24, f32[8,128]{1,0:T(8,128)} %bitcast.25, bf16[128,2048]{1,0:T(8,128)(2,1)} %bitcast.22, f32[1,2048]{1,0:T(1,128)} %norm_ref.1, bf16[2048,16,128]{2,1,0:T(8,128)(2,1)} %bitcast.17, ...), custom_call_target="tpu_custom_call" | custom-call | tf_op jit(solution)/shard_map/stage/pallas_call | solution.py:333
  79.9 0.8 copy.12

commit v11 on v10

--- a/solution.py
+++ b/solution.py
@@ -98,6 +98,10 @@
                 wait(held1[c].at[r1 - 1], recv1.at[c, r1])
             send(from_first(c, r1, {d: to_b[d]}), held2[c].at[r1, 2], send_sem.at[1, c], recv2.at[c, r1, 3], (stage, near_b[d]))
             send(from_first(c, r1, {d: far[d]}), tie2[c].at[r1], send_sem.at[1, c], recv2.at[c, r1, 0], (stage, near_a[d]))
+
+    def direct2(r1):
+        for c in range(COLORS):
+            d = ORDERS[c][1]
             send(from_first(c, r1, {d: to_a[d]}), held2[c].at[r1, 0], send_sem.at[1, c], recv2.at[c, r1, 1], (stage, near_a[d]))
 
     def forward2(r1):
@@ -258,6 +262,7 @@
     phase1()
     side.start()
     phase2(0)
+    direct2(0)
     for copy in local + own:
         copy.start()
     build_gates()
@@ -266,12 +271,15 @@
     flatten(0, pieces // 4, pieces)
     forward1(1)
     phase2(3)
+    direct2(3)
     flatten(1, 0, pieces)
     forward2(0)
     phase2(1)
+    phase2(2)
+    direct2(1)
+    direct2(2)
     flatten(2, 0, pieces // 2)
     forward2(3)
-    phase2(2)
     flatten(2, pieces // 2, pieces)
     forward2(1)
     for copy in own:

time: 81.2 us -> 81.2 us (level)
  no operation moved by 1% of the time
where the time goes in v11:
time: 81.2 us; the launch traced here: 80.7 us
  Pallas kernels  79.9 us (98%)
    pallas_call x1, Pallas kernels, run_stage(): pl.pallas_call(stage_kernel, out_shape=pltpu.VMEM((seq, d), jnp.bfloat16)...  79.9 us

profile of v11, /device:TPU:1, one launch (start us, length us, event | category | flops | bytes accessed | tf_op | source)
XLA Modules:
  0.0 80.7 jit_solution(2654627153539596350)
XLA Ops:
  0.0 79.9 %stage.1 = bf16[128,2048]{1,0:T(8,128)(2,1)S(1)} custom-call(bf16[4,4,4,24,2048]{4,3,2,1,0:T(8,128)(2,1)} %bitcast.21, s32[8,128]{1,0:T(8,128)} %bitcast.23, s32[8,128]{1,0:T(8,128)} %bitcast.24, f32[8,128]{1,0:T(8,128)} %bitcast.25, bf16[128,2048]{1,0:T(8,128)(2,1)} %bitcast.22, f32[1,2048]{1,0:T(1,128)} %norm_ref.1, bf16[2048,16,128]{2,1,0:T(8,128)(2,1)} %bitcast.17, ...), custom_call_target="tpu_custom_call" | custom-call | tf_op jit(solution)/shard_map/stage/pallas_call | solution.py:341
  79.9 0.8 copy.12

commit v12 on v11

--- a/solution.py
+++ b/solution.py
@@ -265,26 +265,27 @@
     direct2(0)
     for copy in local + own:
         copy.start()
-    build_gates()
-    flatten(0, 0, pieces // 4)
+    flatten(0, 0, 3 * pieces // 4)
     forward1(0)
-    flatten(0, pieces // 4, pieces)
+    flatten(0, 3 * pieces // 4, pieces)
     forward1(1)
     phase2(3)
     direct2(3)
-    flatten(1, 0, pieces)
+    build_gates()
+    flatten(1, 0, 3 * pieces // 4)
     forward2(0)
     phase2(1)
     phase2(2)
     direct2(1)
     direct2(2)
-    flatten(2, 0, pieces // 2)
+    flatten(1, 3 * pieces // 4, pieces)
+    flatten(2, 0, pieces // 4)
     forward2(3)
-    flatten(2, pieces // 2, pieces)
+    flatten(2, pieces // 4, 3 * pieces // 4)
     forward2(1)
+    forward2(2)
     for copy in own:
         copy.wait()
-    forward2(2)
     for c in range(COLORS):
         for r1 in range(4):
             for r2 in (1, 2, 3):
@@ -297,6 +298,7 @@
                 send_sums(*before)
             before = (c, role)
     send_sums(*before)
+    flatten(2, 3 * pieces // 4, pieces)
     before = None
     for low in (True, False):
         for c in range(COLORS):

time: 81.2 us -> 81.2 us (level)
  no operation moved by 1% of the time
where the time goes in v12:
time: 81.2 us; the launch traced here: 80.7 us
  Pallas kernels  79.9 us (98%)
    pallas_call x1, Pallas kernels, run_stage(): pl.pallas_call(stage_kernel, out_shape=pltpu.VMEM((seq, d), jnp.bfloat16)...  79.9 us

profile of v12, /device:TPU:1, one launch (start us, length us, event | category | flops | bytes accessed | tf_op | source)
XLA Modules:
  0.0 80.7 jit_solution(17394321878296384934)
XLA Ops:
  0.0 79.9 %stage.1 = bf16[128,2048]{1,0:T(8,128)(2,1)S(1)} custom-call(bf16[4,4,4,24,2048]{4,3,2,1,0:T(8,128)(2,1)} %bitcast.21, s32[8,128]{1,0:T(8,128)} %bitcast.23, s32[8,128]{1,0:T(8,128)} %bitcast.24, f32[8,128]{1,0:T(8,128)} %bitcast.25, bf16[128,2048]{1,0:T(8,128)(2,1)} %bitcast.22, f32[1,2048]{1,0:T(1,128)} %norm_ref.1, bf16[2048,16,128]{2,1,0:T(8,128)(2,1)} %bitcast.17, ...), custom_call_target="tpu_custom_call" | custom-call | tf_op jit(solution)/shard_map/stage/pallas_call | solution.py:343
  79.9 0.8 copy.12

commit v13 on v12

--- a/solution.py
+++ b/solution.py
@@ -286,22 +286,21 @@
     forward2(2)
     for copy in own:
         copy.wait()
+    before = None
     for c in range(COLORS):
         for r1 in range(4):
             for r2 in (1, 2, 3):
                 wait(held2[c].at[r1, r2 - 1], recv2.at[c, r1, r2])
-    before = None
-    for role in (2, 3, 1, 0):
-        for c in range(COLORS):
+        for role in (2, 3, 1, 0):
             partial(c, role)
             if before is not None:
                 send_sums(*before)
             before = (c, role)
+    flatten(2, 3 * pieces // 4, pieces)
     send_sums(*before)
-    flatten(2, 3 * pieces // 4, pieces)
     before = None
-    for low in (True, False):
-        for c in range(COLORS):
+    for c in range(COLORS):
+        for low in (True, False):
             merge(c, low)
             if before is not None:
                 send_merged(*before)

time: 81.2 us -> 82.3 us (1.014)
  Pallas kernels: 79.9 us -> 81 us
    pallas_call x1, Pallas kernels: 79.9 us -> 81 us  [run_stage(): pl.pallas_call(stage_kernel, out_shape=pltpu.VMEM((seq, d), jnp.bfloat16)...]
where the time goes in v13:
time: 82.3 us; the launch traced here: 81.8 us
  Pallas kernels  81 us (98%)
    pallas_call x1, Pallas kernels, run_stage(): pl.pallas_call(stage_kernel, out_shape=pltpu.VMEM((seq, d), jnp.bfloat16)...  81 us

profile of v13, /device:TPU:1, one launch (start us, length us, event | category | flops | bytes accessed | tf_op | source)
XLA Modules:
  0.0 81.8 jit_solution(10154642086191871650)
XLA Ops:
  0.0 81.0 %stage.1 = bf16[128,2048]{1,0:T(8,128)(2,1)S(1)} custom-call(bf16[4,4,4,24,2048]{4,3,2,1,0:T(8,128)(2,1)} %bitcast.21, s32[8,128]{1,0:T(8,128)} %bitcast.23, s32[8,128]{1,0:T(8,128)} %bitcast.24, f32[8,128]{1,0:T(8,128)} %bitcast.25, bf16[128,2048]{1,0:T(8,128)(2,1)} %bitcast.22, f32[1,2048]{1,0:T(1,128)} %norm_ref.1, bf16[2048,16,128]{2,1,0:T(8,128)(2,1)} %bitcast.17, ...), custom_call_target="tpu_custom_call" | custom-call | tf_op jit(solution)/shard_map/stage/pallas_call | solution.py:342
  81.0 0.8 copy.12
